TPU v7x, 128 devices: a whole 4x4x4 slice. The times are simulated.
128 devices in a mesh: depth: 4 (over z), col: 4 (over y), row: 8 (over x, core).
Axes of the slice: x: 4, y: 4, z: 4, core: 2. Of those that a mesh axis runs over, the one named last changes fastest.
Arguments:
- reach_in: bfloat16 [6144, 6144], P(('row', 'depth'), 'col')
Outputs:
- output: bfloat16 [6144, 6144], P(('row', 'depth'), 'col')
All inputs are finite; a program needn't handle non-finite values.
Results may differ from a plain program's by a relative error of at most 0.001.
Values are sent between devices in bfloat16 or wider.
A program may use at most 1 GiB of HBM per device.

v0:
```python
import jax
import jax.numpy as jnp
from jax import lax
from jax.sharding import PartitionSpec as P

SQUARINGS = 4


def solution(mesh):
    depth_size = mesh.shape['depth']
    col_size = mesh.shape['col']
    row_size = mesh.shape['row']
    col_ratio = row_size // col_size
    per_layer = row_size // depth_size
    n_used = min(col_ratio, per_layer)
    all_axes = ('depth', 'col', 'row')

    def linear(layer_id, col_id, row_id):
        return (layer_id * col_size + col_id) * row_size + row_id

    def a_perm(piece_id):
        perm_pairs = []
        for layer_id in range(depth_size):
            for col_id in range(col_size):
                for row_id in range(row_size):
                    offset = (row_id + layer_id * per_layer + piece_id) // col_ratio
                    perm_pairs.append((linear(layer_id, col_id, row_id), linear(layer_id, (col_id - offset) % col_size, row_id)))
        return perm_pairs

    def b_perm():
        perm_pairs = []
        for layer_id in range(depth_size):
            for col_id in range(col_size):
                for k_id in range(row_size):
                    dest_row = (k_id - col_id * col_ratio - layer_id * per_layer) % row_size
                    perm_pairs.append((linear(layer_id, col_id, k_id), linear(layer_id, col_id, dest_row)))
        return perm_pairs

    a_perms = [a_perm(piece_id) for piece_id in range(n_used)]
    b_skew = b_perm()
    col_shift = [(col_id, (col_id - 1) % col_size) for col_id in range(col_size)]
    row_shift = [(row_id, (row_id - 1) % row_size) for row_id in range(row_size)]

    def local_squarings(row_slab):
        row_idx = lax.axis_index('row')
        layer_idx = lax.axis_index('depth')
        for _ in range(SQUARINGS):
            full_block = lax.all_gather(row_slab, 'depth', axis=0, tiled=True)
            k_width = full_block.shape[0]
            window = []
            for piece_id in range(n_used):
                if col_ratio == 1:
                    a_piece = full_block
                else:
                    sub_idx = (row_idx + layer_idx * per_layer + piece_id) % col_ratio
                    a_piece = lax.dynamic_slice_in_dim(full_block, sub_idx * k_width, k_width, axis=1)
                window.append(lax.ppermute(a_piece, all_axes, a_perms[piece_id]))
            b_block = lax.ppermute(full_block, all_axes, b_skew)
            partial_sum = None
            for step_id in range(per_layer):
                slot_id = step_id % col_ratio
                product = jnp.dot(window[slot_id], b_block, preferred_element_type=jnp.float32)
                partial_sum = product if partial_sum is None else partial_sum + product
                if step_id + col_ratio < per_layer:
                    window[slot_id] = lax.ppermute(window[slot_id], 'col', col_shift)
                if step_id + 1 < per_layer:
                    b_block = lax.ppermute(b_block, 'row', row_shift)
            reduced = lax.psum_scatter(partial_sum, 'depth', scatter_dimension=0, tiled=True)
            row_slab = jnp.minimum(reduced + row_slab.astype(jnp.float32), 1.0).astype(jnp.bfloat16)
        return row_slab

    layout = P(('row', 'depth'), 'col')
    return jax.shard_map(local_squarings, mesh=mesh, in_specs=(layout,), out_specs=layout, check_vma=False)
```

profile of v0, /device:TPU:1, one launch (start us, length us, event | category | flops | bytes accessed | tf_op | source)
XLA Modules:
  0.0 838.3 jit_solution(1561355629410007657)
XLA Ops:
  7.3 37.5 %all-gather.5.cloned.1.call-done = bf16[768,1536]{1,0:T(8,128)(2,1)} async-done(((bf16[192,1536]{1,0:T(8,128)(2,1)}), bf16[768,1536]{1,0:T(8,128)(2,1)}) %all-gather.5.cloned.1.call-update) | async-done | bytes 2359312 | tf_op jit(solution)/shard_map/all_gather | solution.py:48
  44.8 2.3 collective-permute-start.1
  50.6 57.9 %collective-permute-start.2 = (bf16[768,768]{1,0:T(8,128)(2,1)S(1)}, bf16[768,768]{1,0:T(8,128)(2,1)S(1)}, u32[]{:S(2)}, u32[]{:S(2)}) collective-permute-start(bf16[768,768]{1,0:T(8,128)(2,1)S(1)} %get-tuple-element.11), channel_id=1, source_target_pairs={{0,0},{1,25},{2,26},{3,19},{4,20},{5,13},{6,14},{7,7},{8,8},{9,1},... | collective-permute-start | bytes 3538952 | tf_op jit(solution)/shard_map/ppermute | solution.py:57
  108.5 2.0 fusion
  110.5 11.1 %collective-permute-done.2 = bf16[768,768]{1,0:T(8,128)(2,1)S(1)} collective-permute-done((bf16[768,768]{1,0:T(8,128)(2,1)S(1)}, bf16[768,768]{1,0:T(8,128)(2,1)S(1)}, u32[]{:S(2)}, u32[]{:S(2)}) %collective-permute-start.2) | collective-permute-done | bytes 1179680 | tf_op jit(solution)/shard_map/ppermute | solution.py:57
  121.6 5.8 convolution_add_fusion.3
  127.4 88.6 %reduce-scatter.5.cloned.1.call-done = f32[192,1536]{1,0:T(8,128)} async-done(((f32[768,1536]{1,0:T(8,128)}), f32[192,1536]{1,0:T(8,128)}) %reduce-scatter.5.cloned.1.call-update) | async-done | bytes 1179664 | tf_op jit(solution)/shard_map/reduce_scatter | solution.py:68
  216.1 2.2 minimum_convert_fusion.3
  218.4 32.5 %all-gather.7.cloned.1.call-done = bf16[768,1536]{1,0:T(8,128)(2,1)} async-done(((bf16[192,1536]{1,0:T(8,128)(2,1)}), bf16[768,1536]{1,0:T(8,128)(2,1)}) %all-gather.7.cloned.1.call-update) | async-done | bytes 2359312 | tf_op jit(solution)/shard_map/all_gather | solution.py:48
  250.9 2.3 collective-permute-start.5
  256.6 57.9 %collective-permute-start.6 = (bf16[768,768]{1,0:T(8,128)(2,1)S(1)}, bf16[768,768]{1,0:T(8,128)(2,1)S(1)}, u32[]{:S(2)}, u32[]{:S(2)}) collective-permute-start(bf16[768,768]{1,0:T(8,128)(2,1)S(1)} %get-tuple-element.9), channel_id=1, source_target_pairs={{0,0},{1,25},{2,26},{3,19},{4,20},{5,13},{6,14},{7,7},{8,8},{9,1},... | collective-permute-start | bytes 3538952 | tf_op jit(solution)/shard_map/ppermute | solution.py:57
  314.5 2.0 fusion.1
  316.5 11.1 %collective-permute-done.6 = bf16[768,768]{1,0:T(8,128)(2,1)S(1)} collective-permute-done((bf16[768,768]{1,0:T(8,128)(2,1)S(1)}, bf16[768,768]{1,0:T(8,128)(2,1)S(1)}, u32[]{:S(2)}, u32[]{:S(2)}) %collective-permute-start.6) | collective-permute-done | bytes 1179680 | tf_op jit(solution)/shard_map/ppermute | solution.py:57
  327.6 4.1 convolution_add_fusion.2
  331.8 88.6 %reduce-scatter.7.cloned.1.call-done = f32[192,1536]{1,0:T(8,128)} async-done(((f32[768,1536]{1,0:T(8,128)}), f32[192,1536]{1,0:T(8,128)}) %reduce-scatter.7.cloned.1.call-update) | async-done | bytes 1179664 | tf_op jit(solution)/shard_map/reduce_scatter | solution.py:68
  420.4 2.2 minimum_convert_fusion.2
  422.7 32.5 %all-gather.9.cloned.1.call-done = bf16[768,1536]{1,0:T(8,128)(2,1)} async-done(((bf16[192,1536]{1,0:T(8,128)(2,1)}), bf16[768,1536]{1,0:T(8,128)(2,1)}) %all-gather.9.cloned.1.call-update) | async-done | bytes 2359312 | tf_op jit(solution)/shard_map/all_gather | solution.py:48
  455.2 2.3 collective-permute-start.9
  461.0 57.9 %collective-permute-start.10 = (bf16[768,768]{1,0:T(8,128)(2,1)S(1)}, bf16[768,768]{1,0:T(8,128)(2,1)S(1)}, u32[]{:S(2)}, u32[]{:S(2)}) collective-permute-start(bf16[768,768]{1,0:T(8,128)(2,1)S(1)} %get-tuple-element.7), channel_id=1, source_target_pairs={{0,0},{1,25},{2,26},{3,19},{4,20},{5,13},{6,14},{7,7},{8,8},{9,1},... | collective-permute-start | bytes 3538952 | tf_op jit(solution)/shard_map/ppermute | solution.py:57
  518.9 2.0 fusion.2
  520.9 11.1 %collective-permute-done.10 = bf16[768,768]{1,0:T(8,128)(2,1)S(1)} collective-permute-done((bf16[768,768]{1,0:T(8,128)(2,1)S(1)}, bf16[768,768]{1,0:T(8,128)(2,1)S(1)}, u32[]{:S(2)}, u32[]{:S(2)}) %collective-permute-start.10) | collective-permute-done | bytes 1179680 | tf_op jit(solution)/shard_map/ppermute | solution.py:57
  532.0 4.1 convolution_add_fusion.1
  536.2 88.6 %reduce-scatter.9.cloned.1.call-done = f32[192,1536]{1,0:T(8,128)} async-done(((f32[768,1536]{1,0:T(8,128)}), f32[192,1536]{1,0:T(8,128)}) %reduce-scatter.9.cloned.1.call-update) | async-done | bytes 1179664 | tf_op jit(solution)/shard_map/reduce_scatter | solution.py:68
  624.8 2.2 minimum_convert_fusion.1
  627.1 32.5 %all-gather.11.cloned.1.call-done = bf16[768,1536]{1,0:T(8,128)(2,1)} async-done(((bf16[192,1536]{1,0:T(8,128)(2,1)}), bf16[768,1536]{1,0:T(8,128)(2,1)}) %all-gather.11.cloned.1.call-update) | async-done | bytes 2359312 | tf_op jit(solution)/shard_map/all_gather | solution.py:48
  659.6 2.3 collective-permute-start.13
  665.4 58.1 %collective-permute-start.14 = (bf16[768,768]{1,0:T(8,128)(2,1)S(1)}, bf16[768,768]{1,0:T(8,128)(2,1)S(1)}, u32[]{:S(2)}, u32[]{:S(2)}) collective-permute-start(bf16[768,768]{1,0:T(8,128)(2,1)S(1)} %get-tuple-element.5), channel_id=1, source_target_pairs={{0,0},{1,25},{2,26},{3,19},{4,20},{5,13},{6,14},{7,7},{8,8},{9,1},... | collective-permute-start | bytes 3538952 | tf_op jit(solution)/shard_map/ppermute | solution.py:57
  723.5 2.0 fusion.3
  725.5 10.9 %collective-permute-done.14 = bf16[768,768]{1,0:T(8,128)(2,1)S(1)} collective-permute-done((bf16[768,768]{1,0:T(8,128)(2,1)S(1)}, bf16[768,768]{1,0:T(8,128)(2,1)S(1)}, u32[]{:S(2)}, u32[]{:S(2)}) %collective-permute-start.14) | collective-permute-done | bytes 1179680 | tf_op jit(solution)/shard_map/ppermute | solution.py:57
  736.4 4.1 convolution_add_fusion
  740.5 88.7 %reduce-scatter.11.cloned.1.call-done = f32[192,1536]{1,0:T(8,128)} async-done(((f32[768,1536]{1,0:T(8,128)}), f32[192,1536]{1,0:T(8,128)}) %reduce-scatter.11.cloned.1.call-update) | async-done | bytes 1179664 | tf_op jit(solution)/shard_map/reduce_scatter | solution.py:68
  829.2 2.2 minimum_convert_fusion
  (48 shorter events, 14.9 us)
Async XLA Ops:
  6.5 38.3 %all-gather.5.cloned.1.call-start = ((), (), s32[]{:S(2)}) async-start(), calls=%async_computation.4 | async-start | bytes 2949120 | tf_op jit(solution)/shard_map/all_gather | solution.py:48
  7.3 208.8 %reduce-scatter.5.cloned.1.call-start = ((), (), s32[]{:S(2)}) async-start(), calls=%async_computation.5 | async-start | bytes 5898240 | tf_op jit(solution)/shard_map/reduce_scatter | solution.py:68
  44.8 2.3 collective-permute-start.1
  47.1 74.5 %collective-permute-start.3 = (bf16[768,1536]{1,0:T(8,128)(2,1)S(1)}, bf16[768,1536]{1,0:T(8,128)(2,1)}, u32[]{:S(2)}, u32[]{:S(2)}) collective-permute-start(bf16[768,1536]{1,0:T(8,128)(2,1)S(1)} %collective-permute-done.1), channel_id=1, source_target_pairs={{0,7},{1,0},{2,1},{3,2},{4,3},{5,4},{6,5},{7,6},{8,15},{9,8},{10,9... | collective-permute-start | bytes 7077896 | tf_op jit(solution)/shard_map/ppermute | solution.py:67
  49.8 58.6 %collective-permute-start = (bf16[768,768]{1,0:T(8,128)(2,1)S(1)}, bf16[768,768]{1,0:T(8,128)(2,1)S(1)}, u32[]{:S(2)}, u32[]{:S(2)}) collective-permute-start(bf16[768,768]{1,0:T(8,128)(2,1)S(1)} %get-tuple-element.12), channel_id=1, source_target_pairs={{0,0},{1,1},{2,26},{3,27},{4,20},{5,21},{6,14},{7,15},{8,8},{9,9},... | collective-permute-start | bytes 3538952 | tf_op jit(solution)/shard_map/ppermute | solution.py:57
  50.6 71.0 %collective-permute-start.2 = (bf16[768,768]{1,0:T(8,128)(2,1)S(1)}, bf16[768,768]{1,0:T(8,128)(2,1)S(1)}, u32[]{:S(2)}, u32[]{:S(2)}) collective-permute-start(bf16[768,768]{1,0:T(8,128)(2,1)S(1)} %get-tuple-element.11), channel_id=1, source_target_pairs={{0,0},{1,25},{2,26},{3,19},{4,20},{5,13},{6,14},{7,7},{8,8},{9,1},... | collective-permute-start | bytes 3538952 | tf_op jit(solution)/shard_map/ppermute | solution.py:57
  127.4 88.7 %copy-start.3 = (bf16[192,1536]{1,0:T(8,128)(2,1)S(1)}, bf16[192,1536]{1,0:T(8,128)(2,1)}, u32[]{:S(2)}) copy-start(bf16[192,1536]{1,0:T(8,128)(2,1)} %param.1) | copy-start | bytes 1769476
  127.4 123.5 %all-gather.7.cloned.1.call-start = ((), (), s32[]{:S(2)}) async-start(), calls=%async_computation.6 | async-start | bytes 2949120 | tf_op jit(solution)/shard_map/all_gather | solution.py:48
  218.3 202.1 %reduce-scatter.7.cloned.1.call-start = ((), (), s32[]{:S(2)}) async-start(), calls=%async_computation.7 | async-start | bytes 5898240 | tf_op jit(solution)/shard_map/reduce_scatter | solution.py:68
  250.9 2.3 collective-permute-start.5
  253.2 74.5 %collective-permute-start.7 = (bf16[768,1536]{1,0:T(8,128)(2,1)S(1)}, bf16[768,1536]{1,0:T(8,128)(2,1)S(1)}, u32[]{:S(2)}, u32[]{:S(2)}) collective-permute-start(bf16[768,1536]{1,0:T(8,128)(2,1)S(1)} %collective-permute-done.5), channel_id=1, source_target_pairs={{0,7},{1,0},{2,1},{3,2},{4,3},{5,4},{6,5},{7,6},{8,15},{9,8},{10,9... | collective-permute-start | bytes 7077896 | tf_op jit(solution)/shard_map/ppermute | solution.py:67
  255.9 58.6 %collective-permute-start.4 = (bf16[768,768]{1,0:T(8,128)(2,1)S(1)}, bf16[768,768]{1,0:T(8,128)(2,1)S(1)}, u32[]{:S(2)}, u32[]{:S(2)}) collective-permute-start(bf16[768,768]{1,0:T(8,128)(2,1)S(1)} %get-tuple-element.10), channel_id=1, source_target_pairs={{0,0},{1,1},{2,26},{3,27},{4,20},{5,21},{6,14},{7,15},{8,8},{9,9},... | collective-permute-start | bytes 3538952 | tf_op jit(solution)/shard_map/ppermute | solution.py:57
  256.6 71.0 %collective-permute-start.6 = (bf16[768,768]{1,0:T(8,128)(2,1)S(1)}, bf16[768,768]{1,0:T(8,128)(2,1)S(1)}, u32[]{:S(2)}, u32[]{:S(2)}) collective-permute-start(bf16[768,768]{1,0:T(8,128)(2,1)S(1)} %get-tuple-element.9), channel_id=1, source_target_pairs={{0,0},{1,25},{2,26},{3,19},{4,20},{5,13},{6,14},{7,7},{8,8},{9,1},... | collective-permute-start | bytes 3538952 | tf_op jit(solution)/shard_map/ppermute | solution.py:57
  331.7 88.7 %copy-start.2 = (bf16[192,1536]{1,0:T(8,128)(2,1)S(1)}, bf16[192,1536]{1,0:T(8,128)(2,1)}, u32[]{:S(2)}) copy-start(bf16[192,1536]{1,0:T(8,128)(2,1)} %minimum_convert_fusion.3) | copy-start | bytes 1769476
  331.8 123.5 %all-gather.9.cloned.1.call-start = ((), (), s32[]{:S(2)}) async-start(), calls=%async_computation.8 | async-start | bytes 2949120 | tf_op jit(solution)/shard_map/all_gather | solution.py:48
  422.7 202.2 %reduce-scatter.9.cloned.1.call-start = ((), (), s32[]{:S(2)}) async-start(), calls=%async_computation.9 | async-start | bytes 5898240 | tf_op jit(solution)/shard_map/reduce_scatter | solution.py:68
  455.2 2.3 collective-permute-start.9
  457.5 74.5 %collective-permute-start.11 = (bf16[768,1536]{1,0:T(8,128)(2,1)S(1)}, bf16[768,1536]{1,0:T(8,128)(2,1)S(1)}, u32[]{:S(2)}, u32[]{:S(2)}) collective-permute-start(bf16[768,1536]{1,0:T(8,128)(2,1)S(1)} %collective-permute-done.9), channel_id=1, source_target_pairs={{0,7},{1,0},{2,1},{3,2},{4,3},{5,4},{6,5},{7,6},{8,15},{9,8},{10,9... | collective-permute-start | bytes 7077896 | tf_op jit(solution)/shard_map/ppermute | solution.py:67
  460.3 58.6 %collective-permute-start.8 = (bf16[768,768]{1,0:T(8,128)(2,1)S(1)}, bf16[768,768]{1,0:T(8,128)(2,1)S(1)}, u32[]{:S(2)}, u32[]{:S(2)}) collective-permute-start(bf16[768,768]{1,0:T(8,128)(2,1)S(1)} %get-tuple-element.8), channel_id=1, source_target_pairs={{0,0},{1,1},{2,26},{3,27},{4,20},{5,21},{6,14},{7,15},{8,8},{9,9},... | collective-permute-start | bytes 3538952 | tf_op jit(solution)/shard_map/ppermute | solution.py:57
  461.0 71.0 %collective-permute-start.10 = (bf16[768,768]{1,0:T(8,128)(2,1)S(1)}, bf16[768,768]{1,0:T(8,128)(2,1)S(1)}, u32[]{:S(2)}, u32[]{:S(2)}) collective-permute-start(bf16[768,768]{1,0:T(8,128)(2,1)S(1)} %get-tuple-element.7), channel_id=1, source_target_pairs={{0,0},{1,25},{2,26},{3,19},{4,20},{5,13},{6,14},{7,7},{8,8},{9,1},... | collective-permute-start | bytes 3538952 | tf_op jit(solution)/shard_map/ppermute | solution.py:57
  536.1 88.7 %copy-start = (bf16[192,1536]{1,0:T(8,128)(2,1)S(1)}, bf16[192,1536]{1,0:T(8,128)(2,1)}, u32[]{:S(2)}) copy-start(bf16[192,1536]{1,0:T(8,128)(2,1)} %minimum_convert_fusion.2) | copy-start | bytes 1769476
  536.2 123.5 %all-gather.11.cloned.1.call-start = ((), (), s32[]{:S(2)}) async-start(), calls=%async_computation.10 | async-start | bytes 2949120 | tf_op jit(solution)/shard_map/all_gather | solution.py:48
  627.1 202.1 %reduce-scatter.11.cloned.1.call-start = ((), (), s32[]{:S(2)}) async-start(), calls=%async_computation.11 | async-start | bytes 5898240 | tf_op jit(solution)/shard_map/reduce_scatter | solution.py:68
  659.6 2.3 collective-permute-start.13
  661.9 74.5 %collective-permute-start.15 = (bf16[768,1536]{1,0:T(8,128)(2,1)S(1)}, bf16[768,1536]{1,0:T(8,128)(2,1)S(1)}, u32[]{:S(2)}, u32[]{:S(2)}) collective-permute-start(bf16[768,1536]{1,0:T(8,128)(2,1)S(1)} %collective-permute-done.13), channel_id=1, source_target_pairs={{0,7},{1,0},{2,1},{3,2},{4,3},{5,4},{6,5},{7,6},{8,15},{9,8},{10,9... | collective-permute-start | bytes 7077896 | tf_op jit(solution)/shard_map/ppermute | solution.py:67
  664.6 58.8 %collective-permute-start.12 = (bf16[768,768]{1,0:T(8,128)(2,1)S(1)}, bf16[768,768]{1,0:T(8,128)(2,1)S(1)}, u32[]{:S(2)}, u32[]{:S(2)}) collective-permute-start(bf16[768,768]{1,0:T(8,128)(2,1)S(1)} %get-tuple-element.6), channel_id=1, source_target_pairs={{0,0},{1,1},{2,26},{3,27},{4,20},{5,21},{6,14},{7,15},{8,8},{9,9},... | collective-permute-start | bytes 3538952 | tf_op jit(solution)/shard_map/ppermute | solution.py:57
  665.4 71.0 %collective-permute-start.14 = (bf16[768,768]{1,0:T(8,128)(2,1)S(1)}, bf16[768,768]{1,0:T(8,128)(2,1)S(1)}, u32[]{:S(2)}, u32[]{:S(2)}) collective-permute-start(bf16[768,768]{1,0:T(8,128)(2,1)S(1)} %get-tuple-element.5), channel_id=1, source_target_pairs={{0,0},{1,25},{2,26},{3,19},{4,20},{5,13},{6,14},{7,7},{8,8},{9,1},... | collective-permute-start | bytes 3538952 | tf_op jit(solution)/shard_map/ppermute | solution.py:57
  740.5 88.7 %copy-start.1 = (bf16[192,1536]{1,0:T(8,128)(2,1)S(1)}, bf16[192,1536]{1,0:T(8,128)(2,1)}, u32[]{:S(2)}) copy-start(bf16[192,1536]{1,0:T(8,128)(2,1)} %minimum_convert_fusion.1) | copy-start | bytes 1769476
Sparse Core Ops, SparseCore 0:
  9.0 35.7 all-gather.4
  127.5 88.5 reduce-scatter.4
  218.4 32.3 all-gather.6
  331.9 88.4 reduce-scatter.6
  422.8 32.3 all-gather.8
  536.3 88.5 reduce-scatter.8
  627.2 32.3 all-gather.10
  740.7 88.5 reduce-scatter.10
where the time goes:
time: 839 us; the launch traced here: 838 us
  waiting for transfers between devices  535 us (64%)
  starting transfers between devices  248 us (30%)
  matrix products  26.1 us (3%)
  between operations  13.6 us (2%)
  other arithmetic  8.89 us (1%)
    reduce_scatter x4, waiting for transfers between devices, local_squarings(): lax.psum_scatter(partial_sum, 'depth', scatter_dimension=0, tiled=True)  355 us
    ppermute x8, starting transfers between devices, local_squarings(): window.append(lax.ppermute(a_piece, all_axes, a_perms[piece_id]))  235 us
    all_gather x4, waiting for transfers between devices, local_squarings(): full_block = lax.all_gather(row_slab, 'depth', axis=0, tiled=True)  135 us
    ppermute x8, waiting for transfers between devices, local_squarings(): window.append(lax.ppermute(a_piece, all_axes, a_perms[piece_id]))  44.3 us
    dot_general x8, matrix products, local_squarings(): jnp.dot(window[slot_id], b_block, preferred_element_type=jnp.float32)  26.1 us
  transfers between devices with their start and end apart: 24, of which 12 were waited for; matrix products, arithmetic and copies ran while one was open for 2% of the time, Pallas kernels for 0%

commit v1 on v0

v1 whole, which is shorter than its diff:
```python
import jax
import jax.numpy as jnp
from jax import lax
from jax.sharding import PartitionSpec as P

SQUARINGS = 4


def solution(mesh):
    depth_size = mesh.shape['depth']
    col_size = mesh.shape['col']
    row_size = mesh.shape['row']
    col_ratio = row_size // col_size

    def local_squarings(row_slab):
        slab, cols = row_slab.shape
        for _ in range(SQUARINGS):
            b_full = lax.all_gather(row_slab, 'row', axis=0, tiled=True)
            a_in = row_slab.reshape(slab, col_ratio, depth_size, slab)
            a_piece = lax.all_to_all(a_in, 'depth', split_axis=2, concat_axis=0, tiled=True)
            a_piece = a_piece.reshape(slab * depth_size, col_ratio * slab)
            a_full = lax.all_gather(a_piece, 'col', axis=1, tiled=True)
            product = jnp.dot(a_full, b_full, preferred_element_type=jnp.float32)
            hits = jnp.minimum(product, 1.0).astype(jnp.bfloat16)
            reduced = lax.psum_scatter(hits, 'depth', scatter_dimension=0, tiled=True)
            total = reduced.astype(jnp.float32) + row_slab.astype(jnp.float32)
            row_slab = jnp.minimum(total, 1.0).astype(jnp.bfloat16)
        return row_slab

    layout = P(('row', 'depth'), 'col')
    return jax.shard_map(local_squarings, mesh=mesh, in_specs=(layout,), out_specs=layout, check_vma=False)
```

time: 839 us -> 528 us (0.63)
  starting transfers between devices: 248 us -> 0.63 us
  waiting for transfers between devices: 535 us -> 404 us
  blocking collectives: 0 us -> 58.3 us
    ppermute x16 -> x0, starting transfers between devices: 248 us -> none  [the longest x8 235 us: local_squarings(): window.append(lax.ppermute(a_piece, all_axes, a_perms[piece_id]))]
    reduce_scatter x4, waiting for transfers between devices: 355 us -> 127 us  [local_squarings(): reduced = lax.psum_scatter(hits, 'depth', scatter_dimension=0, tiled=True)]
    all_gather x4 -> x8, waiting for transfers between devices: 135 us -> 275 us  [the longest x4 145 us: local_squarings(): b_full = lax.all_gather(row_slab, 'row', axis=0, tiled=True)]
    all_to_all x0 -> x4, blocking collectives: none -> 58.3 us  [local_squarings(): lax.all_to_all(a_in, 'depth', split_axis=2, concat_axis=0, tiled=True)]
    ppermute x16 -> x0, waiting for transfers between devices: 44.3 us -> none  [the longest x8 44.3 us: local_squarings(): window.append(lax.ppermute(a_piece, all_axes, a_perms[piece_id]))]
    reshape x0 -> x12, local copies, waits for them, and re-layouts: none -> 12 us  [the longest x8 7.02 us: local_squarings(): a_in = row_slab.reshape(slab, col_ratio, depth_size, slab)]
    dot_general x8 -> x4, matrix products: 26.1 us -> 33.3 us  [local_squarings(): product = jnp.dot(a_full, b_full, preferred_element_type=jnp.float32)]
  transfers between devices with their start and end apart: 24 -> 12, of which waited for: 12 -> 12; matrix products, arithmetic and copies ran while one was open for 2% -> 0% of each run, Pallas kernels for 0% -> 0%
where the time goes in v1:
time: 528 us
  waiting for transfers between devices  404 us (77%)
  blocking collectives  58.3 us (11%)
  matrix products  33.3 us (6%)
  between operations  13.7 us (3%)
  local copies, waits for them, and re-layouts  12 us (2%)
  other arithmetic  5.76 us (1%)
    all_gather x4, waiting for transfers between devices, local_squarings(): b_full = lax.all_gather(row_slab, 'row', axis=0, tiled=True)  145 us
    all_gather x4, waiting for transfers between devices, local_squarings(): a_full = lax.all_gather(a_piece, 'col', axis=1, tiled=True)  129 us
    reduce_scatter x4, waiting for transfers between devices, local_squarings(): reduced = lax.psum_scatter(hits, 'depth', scatter_dimension=0, tiled=True)  127 us
    all_to_all x4, blocking collectives, local_squarings(): lax.all_to_all(a_in, 'depth', split_axis=2, concat_axis=0, tiled=True)  58.3 us
    dot_general x4, matrix products, local_squarings(): product = jnp.dot(a_full, b_full, preferred_element_type=jnp.float32)  33.3 us
  transfers between devices with their start and end apart: 12, of which 12 were waited for; matrix products, arithmetic and copies ran while one was open for 0% of the time, Pallas kernels for 0%

profile of v1, /device:TPU:1, one launch (start us, length us, event | category | flops | bytes accessed | tf_op | source)
XLA Modules:
  0.0 528.0 jit_solution(14553682219881849647)
XLA Ops:
  6.5 2.4 reshape.28
  9.6 17.1 %all_to_all.60 = bf16[192,2,4,192]{3,1,0,2:T(2,128)(2,1)S(1)} all-to-all(bf16[192,2,4,192]{3,1,0,2:T(2,128)(2,1)S(1)} %copy.2), channel_id=1, replica_groups=mesh['depth'=4,'col'=4,'row'=8] {'depth'}, dimensions={2} | all-to-all | bytes 1179648 | tf_op jit(solution)/shard_map/all_to_all | solution.py:20
  26.6 1.2 reshape.29
  28.7 32.4 %all-gather.9.cloned.1.call-done = bf16[768,1536]{1,0:T(8,128)(2,1)} async-done(((bf16[768,384]{1,0:T(8,128)(2,1)}), bf16[768,1536]{1,0:T(8,128)(2,1)}) %all-gather.9.cloned.1.call-update) | async-done | bytes 2359312 | tf_op jit(solution)/shard_map/all_gather | solution.py:22
  61.1 36.4 %all-gather.11.cloned.1.call-done = bf16[1536,1536]{1,0:T(8,128)(2,1)} async-done(((bf16[192,1536]{1,0:T(8,128)(2,1)}), bf16[1536,1536]{1,0:T(8,128)(2,1)}) %all-gather.11.cloned.1.call-update) | async-done | bytes 4718608 | tf_op jit(solution)/shard_map/all_gather | solution.py:18
  97.5 8.3 %minimum_convert_fusion.3 = bf16[768,1536]{1,0:T(8,128)(2,1)} fusion(bf16[768,1536]{1,0:T(8,128)(2,1)} %all-gather.9.cloned.1.call-done, bf16[1536,1536]{1,0:T(8,128)(2,1)} %all-gather.11.cloned.1.call-done), kind=kOutput, calls=%fused_computation.3 | convolution fusion | flops 3626237952 | bytes 9437184 | tf_op jit(solution)/shard_map/dot_general | solution.py:23
  105.9 31.6 %reduce-scatter.5.cloned.1.call-done = bf16[192,1536]{1,0:T(8,128)(2,1)} async-done(((bf16[768,1536]{1,0:T(8,128)(2,1)}), bf16[192,1536]{1,0:T(8,128)(2,1)}) %reduce-scatter.5.cloned.1.call-update) | async-done | bytes 589840 | tf_op jit(solution)/shard_map/reduce_scatter | solution.py:25
  137.5 1.2 minimum_convert_fusion.7
  138.8 0.7 reshape.30
  140.1 13.8 %all_to_all.61 = bf16[192,2,4,192]{3,1,0,2:T(2,128)(2,1)S(1)} all-to-all(bf16[192,2,4,192]{3,1,0,2:T(2,128)(2,1)S(1)} %copy.3), channel_id=1, replica_groups=mesh['depth'=4,'col'=4,'row'=8] {'depth'}, dimensions={2} | all-to-all | bytes 1179648 | tf_op jit(solution)/shard_map/all_to_all | solution.py:20
  153.9 1.2 reshape.31
  155.8 32.5 %all-gather.13.cloned.1.call-done = bf16[768,1536]{1,0:T(8,128)(2,1)} async-done(((bf16[768,384]{1,0:T(8,128)(2,1)}), bf16[768,1536]{1,0:T(8,128)(2,1)}) %all-gather.13.cloned.1.call-update) | async-done | bytes 2359312 | tf_op jit(solution)/shard_map/all_gather | solution.py:22
  188.3 36.3 %all-gather.15.cloned.1.call-done = bf16[1536,1536]{1,0:T(8,128)(2,1)} async-done(((bf16[192,1536]{1,0:T(8,128)(2,1)}), bf16[1536,1536]{1,0:T(8,128)(2,1)}) %all-gather.15.cloned.1.call-update) | async-done | bytes 4718608 | tf_op jit(solution)/shard_map/all_gather | solution.py:18
  224.6 8.3 %minimum_convert_fusion.2 = bf16[768,1536]{1,0:T(8,128)(2,1)} fusion(bf16[768,1536]{1,0:T(8,128)(2,1)} %all-gather.13.cloned.1.call-done, bf16[1536,1536]{1,0:T(8,128)(2,1)} %all-gather.15.cloned.1.call-done), kind=kOutput, calls=%fused_computation.2 | convolution fusion | flops 3626237952 | bytes 9437184 | tf_op jit(solution)/shard_map/dot_general | solution.py:23
  233.0 31.6 %reduce-scatter.7.cloned.1.call-done = bf16[192,1536]{1,0:T(8,128)(2,1)} async-done(((bf16[768,1536]{1,0:T(8,128)(2,1)}), bf16[192,1536]{1,0:T(8,128)(2,1)}) %reduce-scatter.7.cloned.1.call-update) | async-done | bytes 589840 | tf_op jit(solution)/shard_map/reduce_scatter | solution.py:25
  264.6 1.2 minimum_convert_fusion.6
  265.9 0.7 reshape.32
  267.2 13.7 %all_to_all.62 = bf16[192,2,4,192]{3,1,0,2:T(2,128)(2,1)S(1)} all-to-all(bf16[192,2,4,192]{3,1,0,2:T(2,128)(2,1)S(1)} %copy.4), channel_id=1, replica_groups=mesh['depth'=4,'col'=4,'row'=8] {'depth'}, dimensions={2} | all-to-all | bytes 1179648 | tf_op jit(solution)/shard_map/all_to_all | solution.py:20
  281.0 1.2 reshape.33
  283.2 32.2 %all-gather.17.cloned.1.call-done = bf16[768,1536]{1,0:T(8,128)(2,1)} async-done(((bf16[768,384]{1,0:T(8,128)(2,1)}), bf16[768,1536]{1,0:T(8,128)(2,1)}) %all-gather.17.cloned.1.call-update) | async-done | bytes 2359312 | tf_op jit(solution)/shard_map/all_gather | solution.py:22
  315.4 36.4 %all-gather.19.cloned.1.call-done = bf16[1536,1536]{1,0:T(8,128)(2,1)} async-done(((bf16[192,1536]{1,0:T(8,128)(2,1)}), bf16[1536,1536]{1,0:T(8,128)(2,1)}) %all-gather.19.cloned.1.call-update) | async-done | bytes 4718608 | tf_op jit(solution)/shard_map/all_gather | solution.py:18
  351.8 8.3 %minimum_convert_fusion.1 = bf16[768,1536]{1,0:T(8,128)(2,1)} fusion(bf16[768,1536]{1,0:T(8,128)(2,1)} %all-gather.17.cloned.1.call-done, bf16[1536,1536]{1,0:T(8,128)(2,1)} %all-gather.19.cloned.1.call-done), kind=kOutput, calls=%fused_computation.1 | convolution fusion | flops 3626237952 | bytes 9437184 | tf_op jit(solution)/shard_map/dot_general | solution.py:23
  360.2 31.6 %reduce-scatter.9.cloned.1.call-done = bf16[192,1536]{1,0:T(8,128)(2,1)} async-done(((bf16[768,1536]{1,0:T(8,128)(2,1)}), bf16[192,1536]{1,0:T(8,128)(2,1)}) %reduce-scatter.9.cloned.1.call-update) | async-done | bytes 589840 | tf_op jit(solution)/shard_map/reduce_scatter | solution.py:25
  391.9 1.2 minimum_convert_fusion.5
  393.1 0.7 reshape.34
  394.5 13.7 %all_to_all.63 = bf16[192,2,4,192]{3,1,0,2:T(2,128)(2,1)S(1)} all-to-all(bf16[192,2,4,192]{3,1,0,2:T(2,128)(2,1)S(1)} %copy.5), channel_id=1, replica_groups=mesh['depth'=4,'col'=4,'row'=8] {'depth'}, dimensions={2} | all-to-all | bytes 1179648 | tf_op jit(solution)/shard_map/all_to_all | solution.py:20
  408.2 1.2 reshape.35
  410.3 32.4 %all-gather.21.cloned.1.call-done = bf16[768,1536]{1,0:T(8,128)(2,1)} async-done(((bf16[768,384]{1,0:T(8,128)(2,1)}), bf16[768,1536]{1,0:T(8,128)(2,1)}) %all-gather.21.cloned.1.call-update) | async-done | bytes 2359312 | tf_op jit(solution)/shard_map/all_gather | solution.py:22
  442.7 36.4 %all-gather.23.cloned.1.call-done = bf16[1536,1536]{1,0:T(8,128)(2,1)} async-done(((bf16[192,1536]{1,0:T(8,128)(2,1)}), bf16[1536,1536]{1,0:T(8,128)(2,1)}) %all-gather.23.cloned.1.call-update) | async-done | bytes 4718608 | tf_op jit(solution)/shard_map/all_gather | solution.py:18
  479.1 8.3 %minimum_convert_fusion = bf16[768,1536]{1,0:T(8,128)(2,1)} fusion(bf16[768,1536]{1,0:T(8,128)(2,1)} %all-gather.21.cloned.1.call-done, bf16[1536,1536]{1,0:T(8,128)(2,1)} %all-gather.23.cloned.1.call-done), kind=kOutput, calls=%fused_computation | convolution fusion | flops 3626237952 | bytes 9437184 | tf_op jit(solution)/shard_map/dot_general | solution.py:23
  487.4 31.7 %reduce-scatter.11.cloned.1.call-done = bf16[192,1536]{1,0:T(8,128)(2,1)} async-done(((bf16[768,1536]{1,0:T(8,128)(2,1)}), bf16[192,1536]{1,0:T(8,128)(2,1)}) %reduce-scatter.11.cloned.1.call-update) | async-done | bytes 589840 | tf_op jit(solution)/shard_map/reduce_scatter | solution.py:25
  519.1 2.1 minimum_convert_fusion.4
  (42 shorter events, 5.8 us)
Async XLA Ops:
  6.5 54.5 %all-gather.9.cloned.1.call-start = ((), (), s32[]{:S(2)}) async-start(), calls=%async_computation.8 | async-start | bytes 2949120 | tf_op jit(solution)/shard_map/all_gather | solution.py:22
  27.9 69.6 %all-gather.11.cloned.1.call-start = ((), (), s32[]{:S(2)}) async-start(), calls=%async_computation.9 | async-start | bytes 5308416 | tf_op jit(solution)/shard_map/all_gather | solution.py:18
  28.7 108.9 %reduce-scatter.5.cloned.1.call-start = ((), (), s32[]{:S(2)}) async-start(), calls=%async_computation.10 | async-start | bytes 2949120 | tf_op jit(solution)/shard_map/reduce_scatter | solution.py:25
  105.8 31.7 %copy-start.6 = (bf16[192,1536]{1,0:T(8,128)(2,1)S(1)}, bf16[192,1536]{1,0:T(8,128)(2,1)}, u32[]{:S(2)}) copy-start(bf16[192,1536]{1,0:T(8,128)(2,1)} %param.1) | copy-start | bytes 1769476
  105.8 82.5 %all-gather.13.cloned.1.call-start = ((), (), s32[]{:S(2)}) async-start(), calls=%async_computation.11 | async-start | bytes 2949120 | tf_op jit(solution)/shard_map/all_gather | solution.py:22
  138.8 16.4 %copy-start.2 = (bf16[192,1536]{1,0:T(8,128)(2,1)}, bf16[192,1536]{1,0:T(8,128)(2,1)S(1)}, u32[]{:S(2)}) copy-start(bf16[192,1536]{1,0:T(8,128)(2,1)S(1)} %minimum_convert_fusion.7) | copy-start | bytes 1769476
  155.2 69.4 %all-gather.15.cloned.1.call-start = ((), (), s32[]{:S(2)}) async-start(), calls=%async_computation.12 | async-start | bytes 5308416 | tf_op jit(solution)/shard_map/all_gather | solution.py:18
  155.7 108.9 %reduce-scatter.7.cloned.1.call-start = ((), (), s32[]{:S(2)}) async-start(), calls=%async_computation.13 | async-start | bytes 2949120 | tf_op jit(solution)/shard_map/reduce_scatter | solution.py:25
  232.9 31.7 %copy-start.3 = (bf16[192,1536]{1,0:T(8,128)(2,1)S(1)}, bf16[192,1536]{1,0:T(8,128)(2,1)}, u32[]{:S(2)}) copy-start(bf16[192,1536]{1,0:T(8,128)(2,1)} %copy-done.2) | copy-start | bytes 1769476
  232.9 82.5 %all-gather.17.cloned.1.call-start = ((), (), s32[]{:S(2)}) async-start(), calls=%async_computation.14 | async-start | bytes 2949120 | tf_op jit(solution)/shard_map/all_gather | solution.py:22
  265.9 16.3 %copy-start = (bf16[192,1536]{1,0:T(8,128)(2,1)}, bf16[192,1536]{1,0:T(8,128)(2,1)S(1)}, u32[]{:S(2)}) copy-start(bf16[192,1536]{1,0:T(8,128)(2,1)S(1)} %minimum_convert_fusion.6) | copy-start | bytes 1769476
  282.2 69.6 %all-gather.19.cloned.1.call-start = ((), (), s32[]{:S(2)}) async-start(), calls=%async_computation.15 | async-start | bytes 5308416 | tf_op jit(solution)/shard_map/all_gather | solution.py:18
  283.0 108.9 %reduce-scatter.9.cloned.1.call-start = ((), (), s32[]{:S(2)}) async-start(), calls=%async_computation.16 | async-start | bytes 2949120 | tf_op jit(solution)/shard_map/reduce_scatter | solution.py:25
  360.1 31.7 %copy-start.1 = (bf16[192,1536]{1,0:T(8,128)(2,1)S(1)}, bf16[192,1536]{1,0:T(8,128)(2,1)}, u32[]{:S(2)}) copy-start(bf16[192,1536]{1,0:T(8,128)(2,1)} %copy-done) | copy-start | bytes 1769476
  360.2 82.5 %all-gather.21.cloned.1.call-start = ((), (), s32[]{:S(2)}) async-start(), calls=%async_computation.17 | async-start | bytes 2949120 | tf_op jit(solution)/shard_map/all_gather | solution.py:22
  393.1 16.3 %copy-start.4 = (bf16[192,1536]{1,0:T(8,128)(2,1)}, bf16[192,1536]{1,0:T(8,128)(2,1)S(1)}, u32[]{:S(2)}) copy-start(bf16[192,1536]{1,0:T(8,128)(2,1)S(1)} %minimum_convert_fusion.5) | copy-start | bytes 1769476
  409.5 69.6 %all-gather.23.cloned.1.call-start = ((), (), s32[]{:S(2)}) async-start(), calls=%async_computation.18 | async-start | bytes 5308416 | tf_op jit(solution)/shard_map/all_gather | solution.py:18
  410.2 108.9 %reduce-scatter.11.cloned.1.call-start = ((), (), s32[]{:S(2)}) async-start(), calls=%async_computation.19 | async-start | bytes 2949120 | tf_op jit(solution)/shard_map/reduce_scatter | solution.py:25
  487.4 31.7 %copy-start.5 = (bf16[192,1536]{1,0:T(8,128)(2,1)S(1)}, bf16[192,1536]{1,0:T(8,128)(2,1)}, u32[]{:S(2)}) copy-start(bf16[192,1536]{1,0:T(8,128)(2,1)} %copy-done.4) | copy-start | bytes 1769476
Sparse Core Ops, SparseCore 0:
  28.0 33.0 all-gather.8
  62.8 34.6 all-gather.10
  106.0 31.5 reduce-scatter.4
  155.3 32.9 all-gather.12
  189.8 34.6 all-gather.14
  233.0 31.5 reduce-scatter.6
  282.3 33.0 all-gather.16
  317.1 34.6 all-gather.18
  360.3 31.5 reduce-scatter.8
  409.6 33.0 all-gather.20
  444.3 34.6 all-gather.22
  487.6 31.5 reduce-scatter.10

commit v2 on v1

v2 whole, which is shorter than its diff:
```python
import jax
import jax.numpy as jnp
from jax import lax
from jax.experimental import pallas as pl
from jax.experimental.pallas import tpu as pltpu
from jax.sharding import PartitionSpec as P

SQUARINGS = 4
CHUNKS = 4
TILE = 512
MESH = pl.DeviceIdType.MESH
F32, BF16 = jnp.float32, jnp.bfloat16
NAMES = (
    's1p', 's1m', 'dp', 'dm', 's2p', 's2m', 'a1', 'a2', 'a3', 'xp', 'xm', 'xfp', 'xfm',
    'yp', 'ym', 'yfp', 'yfm', 'co', 'cl', 'cr', 'cx',
)


def kernel(r_ref, out_ref, a_all, b_all, part, s1_in, s2_in, sums, send_sem, recv_sem, load_sem):
    slab, width = r_ref.shape
    rows = slab // CHUNKS
    piece = width // 4
    half = width // 2
    z, y, r = lax.axis_index('depth'), lax.axis_index('col'), lax.axis_index('row')
    x, core = r // 2, lax.rem(r, 2)

    def ring(i, step):
        return lax.rem(i + step + 4, 4)

    row_of = {step: 2 * ring(x, step) + core for step in (-1, 1, 2)}
    mate = 2 * x + 1 - core
    depth_at = {step: {'depth': ring(z, step)} for step in (-1, 1, 2)}
    col_at = {step: {'col': ring(y, step)} for step in (-1, 1)}
    row_at = {step: {'row': row_of[step]} for step in (-1, 1)}
    core_at = {'row': mate}

    barrier = pltpu.get_barrier_semaphore()
    peers = list(depth_at.values()) + list(col_at.values()) + list(row_at.values()) + [core_at]
    for peer in peers:
        pl.semaphore_signal(barrier, inc=1, device_id=peer, device_id_type=MESH)
    load = pltpu.make_async_copy(r_ref, b_all.at[0, r], load_sem)
    load.start()
    load.wait()
    pl.semaphore_wait(barrier, len(peers))

    pending = {}

    def copy(name, slot, m, src, dst, device):
        index = NAMES.index(name)
        return pltpu.make_async_remote_copy(
            src_ref=src, dst_ref=dst, send_sem=send_sem.at[index, m], recv_sem=recv_sem.at[index, slot, m],
            device_id=device, device_id_type=MESH,
        )

    def send(name, slot, m, src, dst, device):
        flush((name,), m)
        pending[name, m] = copy(name, slot, m, src, dst, device)
        pending[name, m].start()

    def flush(names, m):
        for name in names:
            done = pending.pop((name, m), None)
            if done is not None:
                done.wait_send()

    def arrived(name, slot, m, place):
        copy(name, slot, m, place, place, core_at).wait_recv()

    def span(m):
        return pl.ds(m * rows, rows)

    def b_at(slot, row, m, columns=slice(None)):
        return b_all.at[slot, row, span(m), columns]

    low, high, full = pl.ds(0, half), pl.ds(half, half), slice(None)

    def multiply(t, m):
        slot = t % 2
        if m == 0:
            for c in range(CHUNKS):
                for name, row in (('co', x * 2), ('cl', ring(x, -1) * 2), ('cr', ring(x, 1) * 2), ('cx', ring(x, 2) * 2)):
                    arrived(name, slot, c, b_at(slot, row + 1 - core, c))
        arrived('yfp', slot, m, a_all.at[slot, m, ring(y, 2), pl.ds(0, 2)])
        arrived('yfm', slot, m, a_all.at[slot, m, ring(y, 2), pl.ds(2, 2)])
        flush(('s1p', 's1m', 'dp', 'dm'), m)

        def tile(i, carry):
            columns = pl.ds(pl.multiple_of(i * TILE, TILE), TILE)
            left = jnp.concatenate([a_all[slot, m, q].reshape(4 * rows, piece) for q in range(4)], axis=1)
            right = b_all[slot, :, :, columns].reshape(width, TILE)
            hits = jnp.minimum(jnp.dot(left, right, preferred_element_type=F32), 1.0).astype(BF16)
            part[m, :, :, columns] = hits.reshape(4, rows, TILE)
            return carry

        lax.fori_loop(0, width // TILE, tile, 0)

    def reduce_first(t, m):
        far, up, down = ring(z, 2), ring(z, 1), ring(z, -1)
        send('s1p', t % 2, m, part.at[m, far, :, low], s1_in.at[0, m], depth_at[1])
        send('s1m', t % 2, m, part.at[m, far, :, high], s1_in.at[1, m], depth_at[-1])
        send('dp', t % 2, m, part.at[m, up, :, high], s2_in.at[0, m, :, high], depth_at[1])
        send('dm', t % 2, m, part.at[m, down, :, low], s2_in.at[1, m, :, low], depth_at[-1])

    def reduce_second(t, m):
        up, down = ring(z, 1), ring(z, -1)
        flush(('s2p', 's2m'), m)
        arrived('s1p', t % 2, m, s1_in.at[0, m])
        sums[0, m] = (s1_in[0, m].astype(F32) + part[m, up, :, low].astype(F32)).astype(BF16)
        send('s2p', t % 2, m, sums.at[0, m], s2_in.at[0, m, :, low], depth_at[1])
        arrived('s1m', t % 2, m, s1_in.at[1, m])
        sums[1, m] = (s1_in[1, m].astype(F32) + part[m, down, :, high].astype(F32)).astype(BF16)
        send('s2m', t % 2, m, sums.at[1, m], s2_in.at[1, m, :, high], depth_at[-1])

    def share(slot, m):
        flush(('xfp', 'xfm', 'co', 'cl', 'cr', 'cx'), m)
        here = b_at(slot, r, m)
        for step, name in ((1, 'xp'), (-1, 'xm')):
            send(name, slot, m, here, here, row_at[step])
        for step, name in ((1, 'a1'), (-1, 'a3'), (2, 'a2')):
            columns = pl.ds(pl.multiple_of(ring(z, step) * piece, 128), piece)
            send(name, slot, m, b_at(slot, r, m, columns), a_all.at[slot, m, y, z], depth_at[step])
        send('co', slot, m, here, here, core_at)
        columns = pl.ds(pl.multiple_of(z * piece, 128), piece)
        a_all[slot, m, y, z] = b_all[slot, r, span(m), columns]

    def finish(t, m):
        arrived('dp', t % 2, m, s2_in.at[0, m, :, high])
        arrived('dm', t % 2, m, s2_in.at[1, m, :, low])
        arrived('s2p', t % 2, m, s2_in.at[0, m, :, low])
        arrived('s2m', t % 2, m, s2_in.at[1, m, :, high])
        total = b_all[t % 2, r, span(m), :].astype(F32) + part[m, z].astype(F32)
        total = total + s2_in[0, m].astype(F32) + s2_in[1, m].astype(F32)
        new = jnp.minimum(total, 1.0).astype(BF16)
        if t == SQUARINGS - 1:
            out_ref[span(m), :] = new
        else:
            slot = (t + 1) % 2
            flush(('xp', 'xm', 'a1', 'a2', 'a3', 'co'), m)
            b_all[slot, r, span(m), :] = new
            share(slot, m)

    def pass_rows(slot, m):
        arrived('xp', slot, m, b_at(slot, row_of[-1], m))
        send('xfp', slot, m, b_at(slot, row_of[-1], m, low), b_at(slot, row_of[-1], m, low), row_at[1])
        send('cl', slot, m, b_at(slot, row_of[-1], m), b_at(slot, row_of[-1], m), core_at)
        arrived('xm', slot, m, b_at(slot, row_of[1], m))
        send('xfm', slot, m, b_at(slot, row_of[1], m, high), b_at(slot, row_of[1], m, high), row_at[-1])
        send('cr', slot, m, b_at(slot, row_of[1], m), b_at(slot, row_of[1], m), core_at)

    def pass_far_rows(slot, m):
        arrived('xfp', slot, m, b_at(slot, row_of[2], m, low))
        arrived('xfm', slot, m, b_at(slot, row_of[2], m, high))
        send('cx', slot, m, b_at(slot, row_of[2], m), b_at(slot, row_of[2], m), core_at)

    def start_columns(slot, m):
        flush(('yfp', 'yfm', 'yp', 'ym'), m)
        for step, name in ((-1, 'a1'), (1, 'a3'), (2, 'a2')):
            arrived(name, slot, m, a_all.at[slot, m, y, ring(z, step)])
        mine = a_all.at[slot, m, y]
        send('yp', slot, m, mine, mine, col_at[1])
        send('ym', slot, m, mine, mine, col_at[-1])

    def pass_columns(slot, m):
        before, after = ring(y, -1), ring(y, 1)
        arrived('yp', slot, m, a_all.at[slot, m, before])
        here = a_all.at[slot, m, before, pl.ds(0, 2)]
        send('yfp', slot, m, here, here, col_at[1])
        arrived('ym', slot, m, a_all.at[slot, m, after])
        here = a_all.at[slot, m, after, pl.ds(2, 2)]
        send('yfm', slot, m, here, here, col_at[-1])

    for m in range(CHUNKS):
        share(0, m)
    for k in range(CHUNKS + 1):
        if k < CHUNKS:
            start_columns(0, k)
            pass_rows(0, k)
        if k >= 1:
            pass_columns(0, k - 1)
            pass_far_rows(0, k - 1)

    late = None
    for t in range(SQUARINGS):
        slot = (t + 1) % 2
        for k in range(CHUNKS + 4):
            if k < CHUNKS:
                multiply(t, k)
                reduce_first(t, k)
            if late is not None:
                pass_columns(*late)
                late = None
            if 0 <= k - 1 < CHUNKS:
                reduce_second(t, k - 1)
            if 0 <= k - 2 < CHUNKS:
                finish(t, k - 2)
            if t < SQUARINGS - 1:
                if 0 <= k - 3 < CHUNKS:
                    pass_rows(slot, k - 3)
                    start_columns(slot, k - 3)
                if 0 <= k - 4 < CHUNKS:
                    pass_far_rows(slot, k - 4)
                    if k - 4 < CHUNKS - 1:
                        pass_columns(slot, k - 4)
                    else:
                        late = (slot, k - 4)
    for name, m in list(pending):
        flush((name,), m)


def solution(mesh):
    depth_size = mesh.shape['depth']
    col_ratio = mesh.shape['row'] // mesh.shape['col']

    def local(row_slab):
        slab, width = row_slab.shape
        rows = slab // CHUNKS
        sub = width // (depth_size * col_ratio)
        blocks = row_slab.reshape(slab, col_ratio, depth_size, sub)
        ordered = jnp.swapaxes(blocks, 1, 2).reshape(slab, width)
        out = pl.pallas_call(
            kernel,
            out_shape=jax.ShapeDtypeStruct((slab, width), BF16),
            in_specs=[pl.BlockSpec(memory_space=pl.ANY)],
            out_specs=pl.BlockSpec(memory_space=pltpu.VMEM),
            scratch_shapes=[
                pltpu.VMEM((2, CHUNKS, 4, 4, rows, width // 4), BF16),
                pltpu.VMEM((2, 8, slab, width), BF16),
                pltpu.VMEM((CHUNKS, 4, rows, width), BF16),
                pltpu.VMEM((2, CHUNKS, rows, width // 2), BF16),
                pltpu.VMEM((2, CHUNKS, rows, width), BF16),
                pltpu.VMEM((2, CHUNKS, rows, width // 2), BF16),
                pltpu.SemaphoreType.DMA((len(NAMES), CHUNKS)),
                pltpu.SemaphoreType.DMA((len(NAMES), 2, CHUNKS)),
                pltpu.SemaphoreType.DMA,
            ],
            compiler_params=pltpu.CompilerParams(collective_id=0, has_side_effects=True),
        )(ordered)
        back = jnp.swapaxes(out.reshape(slab, depth_size, col_ratio, sub), 1, 2)
        return back.reshape(slab, width)

    layout = P(('row', 'depth'), 'col')
    return jax.shard_map(local, mesh=mesh, in_specs=(layout,), out_specs=layout, check_vma=False)
```

time: 528 us -> 185 us (0.35)
  waiting for transfers between devices: 404 us -> 0 us
  Pallas kernels: 0 us -> 175 us
  blocking collectives: 58.3 us -> 0 us
  matrix products: 33.3 us -> 0 us
  between operations: 13.7 us -> 0.04 us
  other arithmetic: 5.76 us -> 0 us
    all_gather x8 -> x0, waiting for transfers between devices: 275 us -> none  [the longest x4 145 us: local_squarings(): b_full = lax.all_gather(row_slab, 'row', axis=0, tiled=True)]
    pallas_call x0 -> x1, Pallas kernels: none -> 175 us  [local(): pl.pallas_call(kernel, out_shape=jax.ShapeDtypeStruct((slab, width), BF16...]
    reduce_scatter x4 -> x0, waiting for transfers between devices: 127 us -> none  [local_squarings(): reduced = lax.psum_scatter(hits, 'depth', scatter_dimension=0, tiled=True)]
    all_to_all x4 -> x0, blocking collectives: 58.3 us -> none  [local_squarings(): lax.all_to_all(a_in, 'depth', split_axis=2, concat_axis=0, tiled=True)]
    dot_general x4 -> x0, matrix products: 33.3 us -> none  [local_squarings(): product = jnp.dot(a_full, b_full, preferred_element_type=jnp.float32)]
    convert_element_type x4 -> x0, other arithmetic: 5.76 us -> none  [local_squarings(): row_slab = jnp.minimum(total, 1.0).astype(jnp.bfloat16)]
    reshape x12 -> x5, local copies, waits for them, and re-layouts: 12 us -> 9.36 us  [the longest x2 3.21 us: local(): blocks = row_slab.reshape(slab, col_ratio, depth_size, sub)]
  transfers between devices with their start and end apart: 12 -> 0, of which waited for: 12 -> 0; matrix products, arithmetic and copies ran while one was open for 0% -> 0% of each run, Pallas kernels for 0% -> 0%
where the time goes in v2:
time: 185 us
  Pallas kernels  175 us (95%)
  local copies, waits for them, and re-layouts  9.76 us (5%)
    pallas_call x1, Pallas kernels, local(): pl.pallas_call(kernel, out_shape=jax.ShapeDtypeStruct((slab, width), BF16...  175 us

profile of v2, /device:TPU:1, one launch (start us, length us, event | category | flops | bytes accessed | tf_op | source)
XLA Modules:
  0.0 184.8 jit_solution(17963352454259304568)
XLA Ops:
  0.0 2.4 %reshape.12 = bf16[192,2,4,192]{3,2,1,0:T(4,128)(2,1)S(1)} reshape(bf16[192,1536]{1,0:T(8,128)(2,1)} %param.1) | data formatting | bytes 1179648 | tf_op jit(solution)/shard_map/reshape | solution.py:218
  2.4 0.8 copy.5
  3.2 1.4 reshape.13.r_ref
  4.7 175.0 %shard_map.17 = bf16[192,1536]{1,0:T(8,128)(2,1)} custom-call(bf16[192,1536]{1,0:T(8,128)(2,1)} %reshape.13.r_ref), custom_call_target="tpu_custom_call" | custom-call | tf_op jit(solution)/shard_map/pallas_call | solution.py:220
  179.6 3.0 %reshape.14 = bf16[192,4,2,192]{3,2,1,0:T(2,128)(2,1)S(1)} reshape(bf16[192,1536]{1,0:T(8,128)(2,1)} %shard_map.17) | data formatting | bytes 1179648 | tf_op jit(solution)/shard_map/reshape | solution.py:238
  182.7 0.4 copy.3
  183.1 1.7 reshape.15

commit v3 on v2

--- a/solution.py
+++ b/solution.py
@@ -16,7 +16,7 @@
 )
 
 
-def kernel(r_ref, out_ref, a_all, b_all, part, s1_in, s2_in, sums, send_sem, recv_sem, load_sem):
+def kernel(r_ref, out_ref, a_all, b_all, part, s1_in, s2_in, sums, send_sem, recv_sem):
     slab, width = r_ref.shape
     rows = slab // CHUNKS
     piece = width // 4
@@ -38,9 +38,11 @@
     peers = list(depth_at.values()) + list(col_at.values()) + list(row_at.values()) + [core_at]
     for peer in peers:
         pl.semaphore_signal(barrier, inc=1, device_id=peer, device_id_type=MESH)
-    load = pltpu.make_async_copy(r_ref, b_all.at[0, r], load_sem)
-    load.start()
-    load.wait()
+    sub = piece // 2
+    for m in range(CHUNKS):
+        given = r_ref[pl.ds(m * rows, rows), :]
+        parts = [given[:, (h * 4 + b) * sub:(h * 4 + b + 1) * sub] for b in range(4) for h in range(2)]
+        b_all[0, r, pl.ds(m * rows, rows), :] = jnp.concatenate(parts, axis=1)
     pl.semaphore_wait(barrier, len(peers))
 
     pending = {}
@@ -132,7 +134,8 @@
         total = total + s2_in[0, m].astype(F32) + s2_in[1, m].astype(F32)
         new = jnp.minimum(total, 1.0).astype(BF16)
         if t == SQUARINGS - 1:
-            out_ref[span(m), :] = new
+            parts = [new[:, (b * 2 + h) * sub:(b * 2 + h + 1) * sub] for h in range(2) for b in range(4)]
+            out_ref[span(m), :] = jnp.concatenate(parts, axis=1)
         else:
             slot = (t + 1) % 2
             flush(('xp', 'xm', 'a1', 'a2', 'a3', 'co'), m)
@@ -208,19 +211,13 @@
 
 
 def solution(mesh):
-    depth_size = mesh.shape['depth']
-    col_ratio = mesh.shape['row'] // mesh.shape['col']
-
     def local(row_slab):
         slab, width = row_slab.shape
         rows = slab // CHUNKS
-        sub = width // (depth_size * col_ratio)
-        blocks = row_slab.reshape(slab, col_ratio, depth_size, sub)
-        ordered = jnp.swapaxes(blocks, 1, 2).reshape(slab, width)
-        out = pl.pallas_call(
+        return pl.pallas_call(
             kernel,
             out_shape=jax.ShapeDtypeStruct((slab, width), BF16),
-            in_specs=[pl.BlockSpec(memory_space=pl.ANY)],
+            in_specs=[pl.BlockSpec(memory_space=pltpu.VMEM)],
             out_specs=pl.BlockSpec(memory_space=pltpu.VMEM),
             scratch_shapes=[
                 pltpu.VMEM((2, CHUNKS, 4, 4, rows, width // 4), BF16),
@@ -231,12 +228,9 @@
                 pltpu.VMEM((2, CHUNKS, rows, width // 2), BF16),
                 pltpu.SemaphoreType.DMA((len(NAMES), CHUNKS)),
                 pltpu.SemaphoreType.DMA((len(NAMES), 2, CHUNKS)),
-                pltpu.SemaphoreType.DMA,
             ],
             compiler_params=pltpu.CompilerParams(collective_id=0, has_side_effects=True),
-        )(ordered)
-        back = jnp.swapaxes(out.reshape(slab, depth_size, col_ratio, sub), 1, 2)
-        return back.reshape(slab, width)
+        )(row_slab)
 
     layout = P(('row', 'depth'), 'col')
     return jax.shard_map(local, mesh=mesh, in_specs=(layout,), out_specs=layout, check_vma=False)

time: 185 us -> 178 us (0.962)
  local copies, waits for them, and re-layouts: 9.76 us -> 1.92 us
    reshape x5 -> x0, local copies, waits for them, and re-layouts: 9.36 us -> none  [the longest x2 3.21 us: local(): blocks = row_slab.reshape(slab, col_ratio, depth_size, sub)]
    unnamed x0 -> x1, local copies, waits for them, and re-layouts: none -> 1.92 us
where the time goes in v3:
time: 178 us
  Pallas kernels  176 us (99%)
  local copies, waits for them, and re-layouts  1.92 us (1%)
    pallas_call x1, Pallas kernels, local(): pl.pallas_call(kernel, out_shape=jax.ShapeDtypeStruct((slab, width), BF16...  176 us

profile of v3, /device:TPU:1, one launch (start us, length us, event | category | flops | bytes accessed | tf_op | source)
XLA Modules:
  0.0 177.5 jit_solution(4109175983961295085)
XLA Ops:
  0.0 175.6 %shard_map.17 = bf16[192,1536]{1,0:T(8,128)(2,1)} custom-call(bf16[192,1536]{1,0:T(8,128)(2,1)} %r_ref.1), custom_call_target="tpu_custom_call" | custom-call | tf_op jit(solution)/shard_map/pallas_call | solution.py:217
  175.6 1.9 %copy.3 = bf16[192,1536]{1,0:T(8,128)(2,1)} copy(bf16[192,1536]{1,0:T(8,128)(2,1)} %shard_map.17) | data formatting | bytes 1179648

commit v4 on v1

v4 whole, which is shorter than its diff:
```python
import jax
import jax.numpy as jnp
from jax import lax
from jax.experimental import pallas as pl
from jax.experimental.pallas import tpu as pltpu
from jax.sharding import PartitionSpec as P

SQUARINGS = 4
MESH = pl.DeviceIdType.MESH
F32, BF16 = jnp.float32, jnp.bfloat16
ROWS = (48, 48, 48, 48)
COLS = (768, 768)
TILE = 256
FAR_ROWS = ()
FAR_SUMS = ()
BLOCK_NAMES = ('s1p', 's1m', 'dp', 'dm', 's2p', 's2m', 'd2', 'xp', 'xm', 'x2', 'xfp', 'xfm', 'co', 'cl', 'cr', 'cx')
CHUNK_NAMES = ('a1', 'a2', 'a3', 'yp', 'ym', 'yfp', 'yfm')
ORDER = (
    'I000 I001 A000 I010', 'G000 I011 Y000 A010', 'G001 I020 H000 G010', 'I030 H001 Y010 Z000', 'G011 I021 A020 G020',
    'I031 A030 G030 Z010', 'Y020 Y030 G021 H020', 'H011 H010 G031 H030', 'B100 C110 C100 H031', 'H021 B101 C101 C111',
    'Z020 Z030 S100 S110', 'S101 S111 C120 F100', 'C130 C121 F111 S120', 'F110 A110 C131 S130', 'F101 A100 S121 F120',
    'G110 G100 G111 Y110', 'G101 S131 F130 F121', 'H100 Y100 F131 A130', 'H101 Z110 G130 A120', 'H110 G120 H111 G121',
    'Z100 H120 Y120 H121', 'G131 Y130 H130 B200', 'C210 C200 H131 B201', 'C211 C201 Z120 S200', 'S210 S211 Z130 S201',
    'C220 C221 F200 C230', 'F211 F201 A200 C231', 'S221 G200 S220 F210', 'A210 S230 G211 G201', 'Y200 S231 F221 F220',
    'H201 G210 F230 F231', 'Y210 Z200 A230 A220', 'G221 H200 G220 H210', 'H211 G230 Z210 Y220', 'H221 Y230 G231 H220',
    'H230 B300 C300 C310', 'H231 B301 C311 C301', 'S300 Z220 S310 S311', 'Z230 S301 C320 C321', 'F300 F310 C330 F301',
    'A300 C331 S320 F311', 'A310 S321 S330 G310', 'Y300 S331 G311 H310', 'G301 F320 F321 F330', 'F331 A330 Y310 H311',
    'H301 A320 Z300 G320', 'G300 G330 Z310 H320', 'G331 H300 G321 Y320', 'Y330 H330 B400 C400', 'C410 H321 H331 B401',
    'C411 C401 Z320 S410', 'S400 Z330 S411 S401', 'C421 C420 C430 C431', 'F400 F411 S420 F410', 'S430 S421 S431 F430',
    'F421 F401 F420 F431',
)


def kernel(r_ref, out_ref, b_all, *refs):
    n = len(ROWS)
    a_all, part, s1_in, s2_in, sums = (refs[i * n:(i + 1) * n] for i in range(5))
    d2_in = refs[5 * n:-4]
    block_send, block_recv, chunk_send, chunk_recv = refs[-4:]
    slab, width = r_ref.shape
    piece, sub = width // 4, width // 8
    z, y, r = lax.axis_index('depth'), lax.axis_index('col'), lax.axis_index('row')
    x, core = r // 2, lax.rem(r, 2)

    def ring(i, step):
        return lax.rem(i + step + 4, 4)

    row_of = {step: 2 * ring(x, step) + core for step in (-1, 1, 2)}
    mate_row = {step: 2 * ring(x, step) + 1 - core for step in (-1, 0, 1, 2)}
    layer = {step: ring(z, step) for step in (-1, 1, 2)}
    block_col = {step: ring(y, step) for step in (-1, 1, 2)}
    depth_at = {step: {'depth': layer[step]} for step in (-1, 1, 2)}
    col_at = {step: {'col': block_col[step]} for step in (-1, 1)}
    row_at = {step: {'row': row_of[step]} for step in (-1, 1, 2)}
    core_at = {'row': mate_row[0]}

    barrier = pltpu.get_barrier_semaphore()
    peers = list(depth_at.values()) + list(col_at.values()) + list(row_at.values()) + [core_at]
    for peer in peers:
        pl.semaphore_signal(barrier, inc=1, device_id=peer, device_id_type=MESH)

    def span(m):
        return pl.ds(sum(ROWS[:m]), ROWS[m])

    def columns(j):
        return pl.ds(sum(COLS[:j]), COLS[j])

    def low(j):
        return pl.ds(sum(COLS[:j]), COLS[j] // 2)

    def high(j):
        return pl.ds(sum(COLS[:j]) + COLS[j] // 2, COLS[j] // 2)

    for m in range(n):
        given = r_ref[span(m), :]
        parts = [given[:, (h * 4 + b) * sub:(h * 4 + b + 1) * sub] for b in range(4) for h in range(2)]
        b_all[0, r, span(m), :] = jnp.concatenate(parts, axis=1)
    pl.semaphore_wait(barrier, len(peers))

    pending = {}
    ready = set()

    def copy(name, slot, m, j, src, dst, device):
        if name in BLOCK_NAMES:
            index, block = BLOCK_NAMES.index(name), m * len(COLS) + j
            sent, landed = block_send.at[index, block], block_recv.at[index, slot, block]
        else:
            index = CHUNK_NAMES.index(name)
            sent, landed = chunk_send.at[index, m], chunk_recv.at[index, slot, m]
        return pltpu.make_async_remote_copy(
            src_ref=src, dst_ref=dst, send_sem=sent, recv_sem=landed, device_id=device, device_id_type=MESH
        )

    def send(name, slot, m, j, src, dst, device):
        flush((name,), m, j)
        pending[name, m, j] = copy(name, slot, m, j, src, dst, device)
        pending[name, m, j].start()

    def flush(names, m, j):
        for name in names:
            done = pending.pop((name, m, j), None)
            if done is not None:
                done.wait_send()

    def arrived(name, slot, m, j, place):
        copy(name, slot, m, j, place, place, core_at).wait_recv()

    def b_at(slot, row, m, cols):
        return b_all.at[slot, row, span(m), cols]

    def take_rows(t, m, j):
        slot = t % 2
        for c in range(n):
            for name, step in (('co', 0), ('cl', -1), ('cr', 1), ('cx', 2)):
                arrived(name, slot, c, j, b_at(slot, mate_row[step], c, columns(j)))

    def multiply(t, m, j):
        slot, rows = t % 2, ROWS[m]
        if (t, m) not in ready:
            ready.add((t, m))
            arrived('yfp', slot, m, 0, a_all[m].at[slot, block_col[2], pl.ds(0, 2)])
            arrived('yfm', slot, m, 0, a_all[m].at[slot, block_col[2], pl.ds(2, 2)])
        flush(('s1p', 's1m', 'dp', 'dm', 'd2'), m, j)
        start = sum(COLS[:j])

        def tile(i, carry):
            cols = pl.ds(pl.multiple_of(start + i * TILE, 128), TILE)
            left = jnp.concatenate([a_all[m][slot, q].reshape(4 * rows, piece) for q in range(4)], axis=1)
            right = b_all[slot, :, :, cols].reshape(width, TILE)
            hits = jnp.minimum(jnp.dot(left, right, preferred_element_type=F32), 1.0).astype(BF16)
            part[m][:, :, cols] = hits.reshape(4, rows, TILE)
            return carry

        lax.fori_loop(0, COLS[j] // TILE, tile, 0)
        mine = part[m]
        if (m, j) in FAR_SUMS:
            send('dp', 0, m, j, mine.at[layer[1], :, columns(j)], s2_in[m].at[0, :, columns(j)], depth_at[1])
            send('dm', 0, m, j, mine.at[layer[-1], :, columns(j)], s2_in[m].at[1, :, columns(j)], depth_at[-1])
            send('d2', 0, m, j, mine.at[layer[2], :, columns(j)], d2_in[m].at[:, columns(j)], depth_at[2])
            return
        send('s1p', 0, m, j, mine.at[layer[2], :, low(j)], s1_in[m].at[:, low(j)], depth_at[1])
        send('s1m', 0, m, j, mine.at[layer[2], :, high(j)], s1_in[m].at[:, high(j)], depth_at[-1])
        send('dp', 0, m, j, mine.at[layer[1], :, high(j)], s2_in[m].at[0, :, high(j)], depth_at[1])
        send('dm', 0, m, j, mine.at[layer[-1], :, low(j)], s2_in[m].at[1, :, low(j)], depth_at[-1])

    def add_passing(t, m, j):
        if (m, j) in FAR_SUMS:
            return
        flush(('s2p', 's2m'), m, j)
        for name, out, side, cols, step in (('s1p', 's2p', 0, low(j), 1), ('s1m', 's2m', 1, high(j), -1)):
            arrived(name, 0, m, j, s1_in[m].at[:, cols])
            total = s1_in[m][:, cols].astype(F32) + part[m][layer[step], :, cols].astype(F32)
            sums[m][:, cols] = total.astype(BF16)
            send(out, 0, m, j, sums[m].at[:, cols], s2_in[m].at[side, :, cols], depth_at[step])

    def share(slot, m, j):
        flush(('xfp', 'xfm', 'cl', 'cr', 'cx'), m, j)
        here = b_at(slot, r, m, columns(j))
        send('xp', slot, m, j, here, here, row_at[1])
        send('xm', slot, m, j, here, here, row_at[-1])
        send('co', slot, m, j, here, here, core_at)
        if (m, j) in FAR_ROWS:
            send('x2', slot, m, j, here, here, row_at[2])

    def share_input(t, m, j):
        share(0, m, j)

    def finish(t, m, j):
        cols = columns(j)
        total = b_all[t % 2, r, span(m), cols].astype(F32) + part[m][z, :, cols].astype(F32)
        if (m, j) in FAR_SUMS:
            arrived('dp', 0, m, j, s2_in[m].at[0, :, cols])
            arrived('dm', 0, m, j, s2_in[m].at[1, :, cols])
            arrived('d2', 0, m, j, d2_in[m].at[:, cols])
            total = total + d2_in[m][:, cols].astype(F32)
        else:
            arrived('dp', 0, m, j, s2_in[m].at[0, :, high(j)])
            arrived('dm', 0, m, j, s2_in[m].at[1, :, low(j)])
            arrived('s2p', 0, m, j, s2_in[m].at[0, :, low(j)])
            arrived('s2m', 0, m, j, s2_in[m].at[1, :, high(j)])
        total = total + s2_in[m][0, :, cols].astype(F32) + s2_in[m][1, :, cols].astype(F32)
        new = jnp.minimum(total, 1.0).astype(BF16)
        if t == SQUARINGS - 1:
            s1_in[m][:, cols] = new
            left[m] -= 1
            if left[m] == 0:
                full = s1_in[m][...]
                parts = [full[:, (b * 2 + h) * sub:(b * 2 + h + 1) * sub] for h in range(2) for b in range(4)]
                out_ref[span(m), :] = jnp.concatenate(parts, axis=1)
        else:
            slot = (t + 1) % 2
            flush(('xp', 'xm', 'x2', 'co'), m, j)
            b_all[slot, r, span(m), cols] = new
            share(slot, m, j)

    def pass_rows(t, m, j):
        slot = (t + 1) % 2
        for name, out, to_mate, step, cols in (('xp', 'xfp', 'cl', -1, low(j)), ('xm', 'xfm', 'cr', 1, high(j))):
            here = b_at(slot, row_of[step], m, columns(j))
            arrived(name, slot, m, j, here)
            if (m, j) not in FAR_ROWS:
                edge = b_at(slot, row_of[step], m, cols)
                send(out, slot, m, j, edge, edge, row_at[-step])
            send(to_mate, slot, m, j, here, here, core_at)

    def pass_far_rows(t, m, j):
        slot = (t + 1) % 2
        here = b_at(slot, row_of[2], m, columns(j))
        if (m, j) in FAR_ROWS:
            arrived('x2', slot, m, j, here)
        else:
            arrived('xfp', slot, m, j, b_at(slot, row_of[2], m, low(j)))
            arrived('xfm', slot, m, j, b_at(slot, row_of[2], m, high(j)))
        send('cx', slot, m, j, here, here, core_at)

    def share_layers(t, m, j):
        slot = (t + 1) % 2
        for step, name in ((1, 'a1'), (-1, 'a3'), (2, 'a2')):
            cols = pl.ds(pl.multiple_of(layer[step] * piece, 128), piece)
            send(name, slot, m, 0, b_at(slot, r, m, cols), a_all[m].at[slot, y, z], depth_at[step])
        cols = pl.ds(pl.multiple_of(z * piece, 128), piece)
        a_all[m][slot, y, z] = b_all[slot, r, span(m), cols]

    def start_columns(t, m, j):
        slot = (t + 1) % 2
        flush(('yfp', 'yfm', 'yp', 'ym'), m, 0)
        for step, name in ((-1, 'a1'), (1, 'a3'), (2, 'a2')):
            arrived(name, slot, m, 0, a_all[m].at[slot, y, layer[step]])
        mine = a_all[m].at[slot, y]
        send('yp', slot, m, 0, mine, mine, col_at[1])
        send('ym', slot, m, 0, mine, mine, col_at[-1])

    def pass_columns(t, m, j):
        slot = (t + 1) % 2
        for name, out, step, start in (('yp', 'yfp', -1, 0), ('ym', 'yfm', 1, 2)):
            arrived(name, slot, m, 0, a_all[m].at[slot, block_col[step]])
            here = a_all[m].at[slot, block_col[step], pl.ds(start, 2)]
            send(out, slot, m, 0, here, here, col_at[-step])

    left = [len(COLS)] * n
    steps = {
        'I': share_input, 'A': share_layers, 'B': take_rows, 'C': multiply, 'S': add_passing, 'F': finish,
        'G': pass_rows, 'H': pass_far_rows, 'Y': start_columns, 'Z': pass_columns,
    }
    for word in ' '.join(ORDER).split():
        t, m, j = (int(digit) for digit in word[1:])
        steps[word[0]](t - 1, m, j)
    for key in list(pending):
        flush(key[:1], *key[1:])


def solution(mesh):
    def local(row_slab):
        slab, width = row_slab.shape
        blocks = len(ROWS) * len(COLS)
        each = lambda shape: [pltpu.VMEM(shape(rows), BF16) for rows in ROWS]
        scratch = [pltpu.VMEM((2, 8, slab, width), BF16)]
        scratch += each(lambda rows: (2, 4, 4, rows, width // 4)) + each(lambda rows: (4, rows, width))
        scratch += each(lambda rows: (rows, width)) + each(lambda rows: (2, rows, width)) + each(lambda rows: (rows, width))
        if FAR_SUMS:
            scratch += each(lambda rows: (rows, width))
        scratch += [
            pltpu.SemaphoreType.DMA((len(BLOCK_NAMES), blocks)),
            pltpu.SemaphoreType.DMA((len(BLOCK_NAMES), 2, blocks)),
            pltpu.SemaphoreType.DMA((len(CHUNK_NAMES), len(ROWS))),
            pltpu.SemaphoreType.DMA((len(CHUNK_NAMES), 2, len(ROWS))),
        ]
        return pl.pallas_call(
            kernel,
            out_shape=jax.ShapeDtypeStruct((slab, width), BF16),
            in_specs=[pl.BlockSpec(memory_space=pltpu.VMEM)],
            out_specs=pl.BlockSpec(memory_space=pltpu.VMEM),
            scratch_shapes=scratch,
            compiler_params=pltpu.CompilerParams(collective_id=0, has_side_effects=True),
        )(row_slab)

    layout = P(('row', 'depth'), 'col')
    return jax.shard_map(local, mesh=mesh, in_specs=(layout,), out_specs=layout, check_vma=False)
```

time: 528 us -> 165 us (0.31)
  waiting for transfers between devices: 404 us -> 0 us
  Pallas kernels: 0 us -> 163 us
  blocking collectives: 58.3 us -> 0 us
  matrix products: 33.3 us -> 0 us
  between operations: 13.7 us -> 0.01 us
  local copies, waits for them, and re-layouts: 12 us -> 1.92 us
  other arithmetic: 5.76 us -> 0 us
    all_gather x8 -> x0, waiting for transfers between devices: 275 us -> none  [the longest x4 145 us: local_squarings(): b_full = lax.all_gather(row_slab, 'row', axis=0, tiled=True)]
    pallas_call x0 -> x1, Pallas kernels: none -> 163 us  [local(): pl.pallas_call(kernel, out_shape=jax.ShapeDtypeStruct((slab, width), BF16...]
    reduce_scatter x4 -> x0, waiting for transfers between devices: 127 us -> none  [local_squarings(): reduced = lax.psum_scatter(hits, 'depth', scatter_dimension=0, tiled=True)]
    all_to_all x4 -> x0, blocking collectives: 58.3 us -> none  [local_squarings(): lax.all_to_all(a_in, 'depth', split_axis=2, concat_axis=0, tiled=True)]
    dot_general x4 -> x0, matrix products: 33.3 us -> none  [local_squarings(): product = jnp.dot(a_full, b_full, preferred_element_type=jnp.float32)]
    reshape x12 -> x0, local copies, waits for them, and re-layouts: 12 us -> none  [the longest x8 7.02 us: local_squarings(): a_in = row_slab.reshape(slab, col_ratio, depth_size, slab)]
    convert_element_type x4 -> x0, other arithmetic: 5.76 us -> none  [local_squarings(): row_slab = jnp.minimum(total, 1.0).astype(jnp.bfloat16)]
  transfers between devices with their start and end apart: 12 -> 0, of which waited for: 12 -> 0; matrix products, arithmetic and copies ran while one was open for 0% -> 0% of each run, Pallas kernels for 0% -> 0%
where the time goes in v4:
time: 165 us
  Pallas kernels  163 us (99%)
  local copies, waits for them, and re-layouts  1.92 us (1%)
    pallas_call x1, Pallas kernels, local(): pl.pallas_call(kernel, out_shape=jax.ShapeDtypeStruct((slab, width), BF16...  163 us

profile of v4, /device:TPU:1, one launch (start us, length us, event | category | flops | bytes accessed | tf_op | source)
XLA Modules:
  0.0 164.8 jit_solution(10169938198630749607)
XLA Ops:
  0.0 162.9 %shard_map.17 = bf16[192,1536]{1,0:T(8,128)(2,1)} custom-call(bf16[192,1536]{1,0:T(8,128)(2,1)} %r_ref.1), custom_call_target="tpu_custom_call" | custom-call | tf_op jit(solution)/shard_map/pallas_call | solution.py:267
  162.9 1.9 %copy.3 = bf16[192,1536]{1,0:T(8,128)(2,1)} copy(bf16[192,1536]{1,0:T(8,128)(2,1)} %shard_map.17) | data formatting | bytes 1179648

commit v5 on v4

--- a/solution.py
+++ b/solution.py
@@ -16,18 +16,14 @@
 BLOCK_NAMES = ('s1p', 's1m', 'dp', 'dm', 's2p', 's2m', 'd2', 'xp', 'xm', 'x2', 'xfp', 'xfm', 'co', 'cl', 'cr', 'cx')
 CHUNK_NAMES = ('a1', 'a2', 'a3', 'yp', 'ym', 'yfp', 'yfm')
 ORDER = (
-    'I000 I001 A000 I010', 'G000 I011 Y000 A010', 'G001 I020 H000 G010', 'I030 H001 Y010 Z000', 'G011 I021 A020 G020',
-    'I031 A030 G030 Z010', 'Y020 Y030 G021 H020', 'H011 H010 G031 H030', 'B100 C110 C100 H031', 'H021 B101 C101 C111',
-    'Z020 Z030 S100 S110', 'S101 S111 C120 F100', 'C130 C121 F111 S120', 'F110 A110 C131 S130', 'F101 A100 S121 F120',
-    'G110 G100 G111 Y110', 'G101 S131 F130 F121', 'H100 Y100 F131 A130', 'H101 Z110 G130 A120', 'H110 G120 H111 G121',
-    'Z100 H120 Y120 H121', 'G131 Y130 H130 B200', 'C210 C200 H131 B201', 'C211 C201 Z120 S200', 'S210 S211 Z130 S201',
-    'C220 C221 F200 C230', 'F211 F201 A200 C231', 'S221 G200 S220 F210', 'A210 S230 G211 G201', 'Y200 S231 F221 F220',
-    'H201 G210 F230 F231', 'Y210 Z200 A230 A220', 'G221 H200 G220 H210', 'H211 G230 Z210 Y220', 'H221 Y230 G231 H220',
-    'H230 B300 C300 C310', 'H231 B301 C311 C301', 'S300 Z220 S310 S311', 'Z230 S301 C320 C321', 'F300 F310 C330 F301',
-    'A300 C331 S320 F311', 'A310 S321 S330 G310', 'Y300 S331 G311 H310', 'G301 F320 F321 F330', 'F331 A330 Y310 H311',
-    'H301 A320 Z300 G320', 'G300 G330 Z310 H320', 'G331 H300 G321 Y320', 'Y330 H330 B400 C400', 'C410 H321 H331 B401',
-    'C411 C401 Z320 S410', 'S400 Z330 S411 S401', 'C421 C420 C430 C431', 'F400 F411 S420 F410', 'S430 S421 S431 F430',
-    'F421 F401 F420 F431',
+    'I0I1A0I2I4I6G0I3A1Y0G1I5A2G2I7A3G4G6Y1Z0H0Y2Y3G3G5G7Z1H4H2H1',
+    'H6B0C0H5Z2H7H3B1C1S0Z3C2S1C4F0S2C6F1A0S4C3G0F2S6C5Y0F4G2S3F6',
+    'H0S5C7F3A1Z0G4H2F5A2S7G6G1G3H4Y1G5F7A3Y2H6B0C0Z1G7H5Y3H3H1S0',
+    'Z2H7B1C1C3F0Z3C2S1C4S3C6S2G0F1A0S4C5S6H0F3F2A1G1C7Y0F4S5G3F6',
+    'Y1S7H1G2F5A2H3Z0G6G4F7A3H2Z1Y2H6H4G5Y3G7B0C2C0H7Z2H5B1S2C1S0',
+    'Z3C3F2S1C4C6S3G2F0F1A0S4S6C5F3A1G0C7Y0G1F6S5G3F4H0Y1S7G6F5A2',
+    'H1H2Z0H3G4F7A3H6Z1G5Y2H4B0G7C0Y3H5C2H7B1S0Z2C3S2C1Z3S3C5F2S1',
+    'C4C6F0C7F1S4S5S6S7F4F3F6F5F7',
 )
 
 
@@ -241,9 +237,14 @@
         'I': share_input, 'A': share_layers, 'B': take_rows, 'C': multiply, 'S': add_passing, 'F': finish,
         'G': pass_rows, 'H': pass_far_rows, 'Y': start_columns, 'Z': pass_columns,
     }
-    for word in ' '.join(ORDER).split():
-        t, m, j = (int(digit) for digit in word[1:])
-        steps[word[0]](t - 1, m, j)
+    order = ''.join(ORDER)
+    turns = {}
+    for code in (order[i:i + 2] for i in range(0, len(order), 2)):
+        name, index = code[0], int(code[1], 16)
+        m, j = (index, 0) if name in 'AYZ' else (0, index) if name == 'B' else divmod(index, len(COLS))
+        t = turns.get(code, -1 if name in 'IAGHYZ' else 0)
+        turns[code] = t + 1
+        steps[name](t, m, j)
     for key in list(pending):
         flush(key[:1], *key[1:])
 

time: 165 us -> 160 us (0.970)
  Pallas kernels: 163 us -> 158 us
    pallas_call x1, Pallas kernels: 163 us -> 158 us  [local(): pl.pallas_call(kernel, out_shape=jax.ShapeDtypeStruct((slab, width), BF16...]
where the time goes in v5:
time: 160 us
  Pallas kernels  158 us (99%)
  local copies, waits for them, and re-layouts  1.92 us (1%)
    pallas_call x1, Pallas kernels, local(): pl.pallas_call(kernel, out_shape=jax.ShapeDtypeStruct((slab, width), BF16...  158 us

profile of v5, /device:TPU:1, one launch (start us, length us, event | category | flops | bytes accessed | tf_op | source)
XLA Modules:
  0.0 159.7 jit_solution(10262510372971311946)
XLA Ops:
  0.0 157.8 %shard_map.17 = bf16[192,1536]{1,0:T(8,128)(2,1)} custom-call(bf16[192,1536]{1,0:T(8,128)(2,1)} %r_ref.1), custom_call_target="tpu_custom_call" | custom-call | tf_op jit(solution)/shard_map/pallas_call | solution.py:268
  157.8 1.9 %copy.3 = bf16[192,1536]{1,0:T(8,128)(2,1)} copy(bf16[192,1536]{1,0:T(8,128)(2,1)} %shard_map.17) | data formatting | bytes 1179648

commit v6 on v5

--- a/solution.py
+++ b/solution.py
@@ -13,8 +13,10 @@
 TILE = 256
 FAR_ROWS = ()
 FAR_SUMS = ()
-BLOCK_NAMES = ('s1p', 's1m', 'dp', 'dm', 's2p', 's2m', 'd2', 'xp', 'xm', 'x2', 'xfp', 'xfm', 'co', 'cl', 'cr', 'cx')
-CHUNK_NAMES = ('a1', 'a2', 'a3', 'yp', 'ym', 'yfp', 'yfm')
+SUM_NAMES = ('s1p', 's1m', 'dp', 'dm', 's2p', 's2m')
+ROW_NAMES = ('xp', 'xm', 'xfp', 'xfm', 'co', 'cl', 'cr', 'cx')
+COL_NAMES = ('a1', 'a2', 'a3', 'yp', 'ym', 'yfp', 'yfm')
+SENDS = 48
 ORDER = (
     'I0I1A0I2I4I6G0I3A1Y0G1I5A2G2I7A3G4G6Y1Z0H0Y2Y3G3G5G7Z1H4H2H1',
     'H6B0C0H5Z2H7H3B1C1S0Z3C2S1C4F0S2C6F1A0S4C3G0F2S6C5Y0F4G2S3F6',
@@ -28,10 +30,21 @@
 
 
 def kernel(r_ref, out_ref, b_all, *refs):
+    blocks = len(ROWS) * len(COLS)
+    pl.run_scoped(
+        lambda *sems: work(r_ref, out_ref, b_all, *refs, *sems),
+        pltpu.SemaphoreType.DMA((SENDS,)),
+        pltpu.SemaphoreType.DMA((len(SUM_NAMES), blocks)),
+        pltpu.SemaphoreType.DMA((len(ROW_NAMES), 2, blocks)),
+        pltpu.SemaphoreType.DMA((len(COL_NAMES), 2, len(ROWS))),
+    )
+
+
+def work(r_ref, out_ref, b_all, *refs):
     n = len(ROWS)
     a_all, part, s1_in, s2_in, sums = (refs[i * n:(i + 1) * n] for i in range(5))
     d2_in = refs[5 * n:-4]
-    block_send, block_recv, chunk_send, chunk_recv = refs[-4:]
+    sent, sum_landed, row_landed, col_landed = refs[-4:]
     slab, width = r_ref.shape
     piece, sub = width // 4, width // 8
     z, y, r = lax.axis_index('depth'), lax.axis_index('col'), lax.axis_index('row')
@@ -73,29 +86,36 @@
     pl.semaphore_wait(barrier, len(peers))
 
     pending = {}
+    free = list(range(SENDS))
     ready = set()
 
-    def copy(name, slot, m, j, src, dst, device):
-        if name in BLOCK_NAMES:
-            index, block = BLOCK_NAMES.index(name), m * len(COLS) + j
-            sent, landed = block_send.at[index, block], block_recv.at[index, slot, block]
-        else:
-            index = CHUNK_NAMES.index(name)
-            sent, landed = chunk_send.at[index, m], chunk_recv.at[index, slot, m]
+    def copy(name, slot, m, j, src, dst, device, out=0):
+        block = m * len(COLS) + j
+        if name in SUM_NAMES:
+            landed = sum_landed.at[SUM_NAMES.index(name), block]
+        elif name in ROW_NAMES:
+            landed = row_landed.at[ROW_NAMES.index(name), slot, block]
+        else:
+            landed = col_landed.at[COL_NAMES.index(name), slot, m]
         return pltpu.make_async_remote_copy(
-            src_ref=src, dst_ref=dst, send_sem=sent, recv_sem=landed, device_id=device, device_id_type=MESH
+            src_ref=src, dst_ref=dst, send_sem=sent.at[out], recv_sem=landed, device_id=device, device_id_type=MESH
         )
 
     def send(name, slot, m, j, src, dst, device):
         flush((name,), m, j)
-        pending[name, m, j] = copy(name, slot, m, j, src, dst, device)
-        pending[name, m, j].start()
+        if not free:
+            oldest = next(iter(pending))
+            flush(oldest[:1], *oldest[1:])
+        out = free.pop(0)
+        pending[name, m, j] = (copy(name, slot, m, j, src, dst, device, out), out)
+        pending[name, m, j][0].start()
 
     def flush(names, m, j):
         for name in names:
             done = pending.pop((name, m, j), None)
             if done is not None:
-                done.wait_send()
+                done[0].wait_send()
+                free.append(done[1])
 
     def arrived(name, slot, m, j, place):
         copy(name, slot, m, j, place, place, core_at).wait_recv()
@@ -252,19 +272,12 @@
 def solution(mesh):
     def local(row_slab):
         slab, width = row_slab.shape
-        blocks = len(ROWS) * len(COLS)
         each = lambda shape: [pltpu.VMEM(shape(rows), BF16) for rows in ROWS]
         scratch = [pltpu.VMEM((2, 8, slab, width), BF16)]
         scratch += each(lambda rows: (2, 4, 4, rows, width // 4)) + each(lambda rows: (4, rows, width))
         scratch += each(lambda rows: (rows, width)) + each(lambda rows: (2, rows, width)) + each(lambda rows: (rows, width))
         if FAR_SUMS:
             scratch += each(lambda rows: (rows, width))
-        scratch += [
-            pltpu.SemaphoreType.DMA((len(BLOCK_NAMES), blocks)),
-            pltpu.SemaphoreType.DMA((len(BLOCK_NAMES), 2, blocks)),
-            pltpu.SemaphoreType.DMA((len(CHUNK_NAMES), len(ROWS))),
-            pltpu.SemaphoreType.DMA((len(CHUNK_NAMES), 2, len(ROWS))),
-        ]
         return pl.pallas_call(
             kernel,
             out_shape=jax.ShapeDtypeStruct((slab, width), BF16),

time: 160 us -> 156 us (0.975); the launches traced: 160 us -> 154 us
  Pallas kernels: 158 us -> 152 us
    pallas_call x1, Pallas kernels: 158 us -> 152 us  [local(): pl.pallas_call(kernel, out_shape=jax.ShapeDtypeStruct((slab, width), BF16...]
where the time goes in v6:
time: 156 us; the launch traced here: 154 us
  Pallas kernels  152 us (97%)
  local copies, waits for them, and re-layouts  1.92 us (1%)
    pallas_call x1, Pallas kernels, local(): pl.pallas_call(kernel, out_shape=jax.ShapeDtypeStruct((slab, width), BF16...  152 us

profile of v6, /device:TPU:1, one launch (start us, length us, event | category | flops | bytes accessed | tf_op | source)
XLA Modules:
  0.0 154.0 jit_solution(13790575229299788178)
XLA Ops:
  0.0 152.1 %shard_map.17 = bf16[192,1536]{1,0:T(8,128)(2,1)} custom-call(bf16[192,1536]{1,0:T(8,128)(2,1)} %r_ref.1), custom_call_target="tpu_custom_call" | custom-call | tf_op jit(solution)/shard_map/pallas_call | solution.py:281
  152.1 1.9 %copy.3 = bf16[192,1536]{1,0:T(8,128)(2,1)} copy(bf16[192,1536]{1,0:T(8,128)(2,1)} %shard_map.17) | data formatting | bytes 1179648

commit v7 on v6

--- a/solution.py
+++ b/solution.py
@@ -18,14 +18,14 @@
 COL_NAMES = ('a1', 'a2', 'a3', 'yp', 'ym', 'yfp', 'yfm')
 SENDS = 48
 ORDER = (
-    'I0I1A0I2I4I6G0I3A1Y0G1I5A2G2I7A3G4G6Y1Z0H0Y2Y3G3G5G7Z1H4H2H1',
-    'H6B0C0H5Z2H7H3B1C1S0Z3C2S1C4F0S2C6F1A0S4C3G0F2S6C5Y0F4G2S3F6',
-    'H0S5C7F3A1Z0G4H2F5A2S7G6G1G3H4Y1G5F7A3Y2H6B0C0Z1G7H5Y3H3H1S0',
-    'Z2H7B1C1C3F0Z3C2S1C4S3C6S2G0F1A0S4C5S6H0F3F2A1G1C7Y0F4S5G3F6',
-    'Y1S7H1G2F5A2H3Z0G6G4F7A3H2Z1Y2H6H4G5Y3G7B0C2C0H7Z2H5B1S2C1S0',
-    'Z3C3F2S1C4C6S3G2F0F1A0S4S6C5F3A1G0C7Y0G1F6S5G3F4H0Y1S7G6F5A2',
-    'H1H2Z0H3G4F7A3H6Z1G5Y2H4B0G7C0Y3H5C2H7B1S0Z2C3S2C1Z3S3C5F2S1',
-    'C4C6F0C7F1S4S5S6S7F4F3F6F5F7',
+    'I1I3I6I2A1I0A0I5Y1I4A2Y0G6G0I7A3Y2G2G4Z0G1H0Z1G5Y3G3G7H2Z2H4',
+    'H6B0C0H3H5H1H7C2B1C3S0Z3C1S2S3C4F0C6S1F2F3A1S4G0S6C7F1A0C5F4',
+    'Y1F6G1S7G2H0Y0S5G4G6F7A3Z1F5A2Z0H1H4H2G7H6Y3G3B0G5C2Y2C0H3H5',
+    'H7B1S2Z3C1C3Z2S0F2S1C6S3C4G2F1S6F0A0S4F3A1C5F6C7Y0H2F4S5G0Y1',
+    'G3S7G6G4F5A2Z0H3F7A3G1H4H0H6Z1G5Y2B0G7C0H1Y3H5C2H7B1S0Z2C1C3',
+    'F0Z3S2S1C5S3C4F2C7F1S5F3G0A1S4A0G2C6G1S7F5Y1F4G3H1S6G5Y0H2F7',
+    'A2G4Z1F6A3G7Z0H0H4Y2H3G6Y3H5H7B1C3H6C1B0C2Z2C0Z3S3S1S2C5C4C7',
+    'C6S0S5S7S4F2S6F0F1F7F5F4F3F6',
 )
 
 

time: 156 us -> 152 us (0.974); the launches traced: 154 us -> 152 us
  Pallas kernels: 152 us -> 150 us
    pallas_call x1, Pallas kernels: 152 us -> 150 us  [local(): pl.pallas_call(kernel, out_shape=jax.ShapeDtypeStruct((slab, width), BF16...]
where the time goes in v7:
time: 152 us
  Pallas kernels  150 us (99%)
  local copies, waits for them, and re-layouts  1.92 us (1%)
    pallas_call x1, Pallas kernels, local(): pl.pallas_call(kernel, out_shape=jax.ShapeDtypeStruct((slab, width), BF16...  150 us

profile of v7, /device:TPU:1, one launch (start us, length us, event | category | flops | bytes accessed | tf_op | source)
XLA Modules:
  0.0 151.8 jit_solution(8568857890090487273)
XLA Ops:
  0.0 149.8 %shard_map.17 = bf16[192,1536]{1,0:T(8,128)(2,1)} custom-call(bf16[192,1536]{1,0:T(8,128)(2,1)} %r_ref.1), custom_call_target="tpu_custom_call" | custom-call | tf_op jit(solution)/shard_map/pallas_call | solution.py:281
  149.8 1.9 %copy.3 = bf16[192,1536]{1,0:T(8,128)(2,1)} copy(bf16[192,1536]{1,0:T(8,128)(2,1)} %shard_map.17) | data formatting | bytes 1179648

commit v8 on v7

--- a/solution.py
+++ b/solution.py
@@ -10,7 +10,7 @@
 F32, BF16 = jnp.float32, jnp.bfloat16
 ROWS = (48, 48, 48, 48)
 COLS = (768, 768)
-TILE = 256
+TILE = 768
 FAR_ROWS = ()
 FAR_SUMS = ()
 SUM_NAMES = ('s1p', 's1m', 'dp', 'dm', 's2p', 's2m')
@@ -18,14 +18,14 @@
 COL_NAMES = ('a1', 'a2', 'a3', 'yp', 'ym', 'yfp', 'yfm')
 SENDS = 48
 ORDER = (
-    'I1I3I6I2A1I0A0I5Y1I4A2Y0G6G0I7A3Y2G2G4Z0G1H0Z1G5Y3G3G7H2Z2H4',
-    'H6B0C0H3H5H1H7C2B1C3S0Z3C1S2S3C4F0C6S1F2F3A1S4G0S6C7F1A0C5F4',
-    'Y1F6G1S7G2H0Y0S5G4G6F7A3Z1F5A2Z0H1H4H2G7H6Y3G3B0G5C2Y2C0H3H5',
-    'H7B1S2Z3C1C3Z2S0F2S1C6S3C4G2F1S6F0A0S4F3A1C5F6C7Y0H2F4S5G0Y1',
-    'G3S7G6G4F5A2Z0H3F7A3G1H4H0H6Z1G5Y2B0G7C0H1Y3H5C2H7B1S0Z2C1C3',
-    'F0Z3S2S1C5S3C4F2C7F1S5F3G0A1S4A0G2C6G1S7F5Y1F4G3H1S6G5Y0H2F7',
-    'A2G4Z1F6A3G7Z0H0H4Y2H3G6Y3H5H7B1C3H6C1B0C2Z2C0Z3S3S1S2C5C4C7',
-    'C6S0S5S7S4F2S6F0F1F7F5F4F3F6',
+    'I1I0A0I3I4I5A2I7I2A1Y0G3G1Y2Y1Z0G5G7I6A3G4Z2G0H3G2H5H1Z1Y3H7',
+    'B1C1G6H4C5C3S1H0H2H6B0C4Z3S5C0S4C7F5F1S0S3F4A2S7G5F0A0F3C2Y2',
+    'C6F7G4Y0S2G1G3S6G7Z2F2A1H1F6H5H7H3G0A3B1Z0G2C5Y1G6Y3H4C1H0H2',
+    'S5H6B0C0C4Z1S1F5Z3S0S4C3F1C7F4A2S3G1G5S7F0A0C6C2F3Y2F7G4S6Y0',
+    'G0S2G3G7Z2F6A3H3F2H5Z0H7A1H1H0B1C5H4Y3G6G2C1Y1S5H6H2B0S1Z3C0',
+    'C4F5Z1F1S0C7S4C3F0A0S7G1S3F4A2C2C6F7Y0F3Y2G0G5S2S6G7G3Z0F2A1',
+    'F6G4Z2A3H5H7H3H1B1C1G2Y1G6C5S1H0Y3H4H2H6B0S5Z1C0C4Z3S0C3C2F5',
+    'S4C7C6S3S2F4S7S6F3F2F1F0F7F6',
 )
 
 

time: 152 us -> 150 us (0.987)
  Pallas kernels: 150 us -> 148 us
    pallas_call x1, Pallas kernels: 150 us -> 148 us  [local(): pl.pallas_call(kernel, out_shape=jax.ShapeDtypeStruct((slab, width), BF16...]
where the time goes in v8:
time: 150 us
  Pallas kernels  148 us (99%)
  local copies, waits for them, and re-layouts  1.92 us (1%)
    pallas_call x1, Pallas kernels, local(): pl.pallas_call(kernel, out_shape=jax.ShapeDtypeStruct((slab, width), BF16...  148 us

profile of v8, /device:TPU:1, one launch (start us, length us, event | category | flops | bytes accessed | tf_op | source)
XLA Modules:
  0.0 149.5 jit_solution(6445315992126423720)
XLA Ops:
  0.0 147.6 %shard_map.17 = bf16[192,1536]{1,0:T(8,128)(2,1)} custom-call(bf16[192,1536]{1,0:T(8,128)(2,1)} %r_ref.1), custom_call_target="tpu_custom_call" | custom-call | tf_op jit(solution)/shard_map/pallas_call | solution.py:281
  147.6 1.9 %copy.3 = bf16[192,1536]{1,0:T(8,128)(2,1)} copy(bf16[192,1536]{1,0:T(8,128)(2,1)} %shard_map.17) | data formatting | bytes 1179648

commit v9 on v8

--- a/solution.py
+++ b/solution.py
@@ -18,14 +18,14 @@
 COL_NAMES = ('a1', 'a2', 'a3', 'yp', 'ym', 'yfp', 'yfm')
 SENDS = 48
 ORDER = (
-    'I1I0A0I3I4I5A2I7I2A1Y0G3G1Y2Y1Z0G5G7I6A3G4Z2G0H3G2H5H1Z1Y3H7',
-    'B1C1G6H4C5C3S1H0H2H6B0C4Z3S5C0S4C7F5F1S0S3F4A2S7G5F0A0F3C2Y2',
-    'C6F7G4Y0S2G1G3S6G7Z2F2A1H1F6H5H7H3G0A3B1Z0G2C5Y1G6Y3H4C1H0H2',
-    'S5H6B0C0C4Z1S1F5Z3S0S4C3F1C7F4A2S3G1G5S7F0A0C6C2F3Y2F7G4S6Y0',
-    'G0S2G3G7Z2F6A3H3F2H5Z0H7A1H1H0B1C5H4Y3G6G2C1Y1S5H6H2B0S1Z3C0',
-    'C4F5Z1F1S0C7S4C3F0A0S7G1S3F4A2C2C6F7Y0F3Y2G0G5S2S6G7G3Z0F2A1',
-    'F6G4Z2A3H5H7H3H1B1C1G2Y1G6C5S1H0Y3H4H2H6B0S5Z1C0C4Z3S0C3C2F5',
-    'S4C7C6S3S2F4S7S6F3F2F1F0F7F6',
+    'I1I0A0I3I7I5I6A3G1Y0Y3G7G3G5I2A1Z0I4A2H7Z3H3G6H1H5G0Y1B1C1G2',
+    'Y2G4C7S1Z1H6H2H0H4S7B0C6C0Z2F1C2S6S0G1C4F7S2F6A3S4F0A0C5C3F2',
+    'Y3G7F4S5Y0G2G0G6S3Z3G4F5A2H1F3H0H2H7Z0A1H6H4B0G5Y2C6G3C0Y1H3',
+    'H5S6Z2S0B1C1C7Z1F0F6S1C4S7C2S4G0F1A0F7S2A3G6C3F4Y0G1C5F2Y3S3',
+    'G4S5G7G2Z0F3A1F5H1H0Z3H6H7H2H4A2G3B0Y1C0G5C6H3Y2S0H5Z1S6B1C1',
+    'C7Z2S1C3F0S7C5F6S3F1A0S5F7A3G0C4F3Y0G6C2F5G7G1Y3S4S2G3Z0G5F4',
+    'A2F2H3A1Z3H7H1H5G4B1Y2C1G2C7Y1H6H0S1H2H4Z2S7B0C6C0Z1S6C5S0F1',
+    'C3F6C2C4S5F0S2S3S4F2F5F3F7F4',
 )
 
 
@@ -194,9 +194,8 @@
             arrived('s2p', 0, m, j, s2_in[m].at[0, :, low(j)])
             arrived('s2m', 0, m, j, s2_in[m].at[1, :, high(j)])
         total = total + s2_in[m][0, :, cols].astype(F32) + s2_in[m][1, :, cols].astype(F32)
-        new = jnp.minimum(total, 1.0).astype(BF16)
         if t == SQUARINGS - 1:
-            s1_in[m][:, cols] = new
+            s1_in[m][:, cols] = total.astype(BF16)
             left[m] -= 1
             if left[m] == 0:
                 full = s1_in[m][...]
@@ -204,6 +203,7 @@
                 out_ref[span(m), :] = jnp.concatenate(parts, axis=1)
         else:
             slot = (t + 1) % 2
+            new = jnp.minimum(total, 1.0).astype(BF16)
             flush(('xp', 'xm', 'x2', 'co'), m, j)
             b_all[slot, r, span(m), cols] = new
             share(slot, m, j)
@@ -278,7 +278,7 @@
         scratch += each(lambda rows: (rows, width)) + each(lambda rows: (2, rows, width)) + each(lambda rows: (rows, width))
         if FAR_SUMS:
             scratch += each(lambda rows: (rows, width))
-        return pl.pallas_call(
+        total = pl.pallas_call(
             kernel,
             out_shape=jax.ShapeDtypeStruct((slab, width), BF16),
             in_specs=[pl.BlockSpec(memory_space=pltpu.VMEM)],
@@ -286,6 +286,7 @@
             scratch_shapes=scratch,
             compiler_params=pltpu.CompilerParams(collective_id=0, has_side_effects=True),
         )(row_slab)
+        return jnp.minimum(total.astype(F32), 1.0).astype(BF16)
 
     layout = P(('row', 'depth'), 'col')
     return jax.shard_map(local, mesh=mesh, in_specs=(layout,), out_specs=layout, check_vma=False)

time: 150 us -> 149 us (level)
  Pallas kernels: 148 us -> 146 us
  other arithmetic: 0 us -> 1.97 us
  local copies, waits for them, and re-layouts: 1.92 us -> 0 us
    convert_element_type x0 -> x1, other arithmetic: none -> 1.97 us  [local(): return jnp.minimum(total.astype(F32), 1.0).astype(BF16)]
    unnamed x1 -> x0, local copies, waits for them, and re-layouts: 1.92 us -> none
where the time goes in v9:
time: 149 us; the launch traced here: 148 us
  Pallas kernels  146 us (98%)
  other arithmetic  1.97 us (1%)
    pallas_call x1, Pallas kernels, local(): pl.pallas_call(kernel, out_shape=jax.ShapeDtypeStruct((slab, width), BF16...  146 us

profile of v9, /device:TPU:1, one launch (start us, length us, event | category | flops | bytes accessed | tf_op | source)
XLA Modules:
  0.0 148.3 jit_solution(1318855197583862073)
XLA Ops:
  0.0 146.3 %shard_map.17 = bf16[192,1536]{1,0:T(8,128)(2,1)} custom-call(bf16[192,1536]{1,0:T(8,128)(2,1)} %r_ref.1), custom_call_target="tpu_custom_call" | custom-call | tf_op jit(solution)/shard_map/pallas_call | solution.py:281
  146.3 2.0 %minimum_convert_fusion = bf16[192,1536]{1,0:T(8,128)(2,1)} fusion(bf16[192,1536]{1,0:T(8,128)(2,1)} %shard_map.17), kind=kLoop, calls=%fused_computation | loop fusion | flops 884736 | bytes 1179648 | tf_op jit(solution)/shard_map/convert_element_type | solution.py:289

commit v10 on v9

--- a/solution.py
+++ b/solution.py
@@ -6,6 +6,7 @@
 from jax.sharding import PartitionSpec as P
 
 SQUARINGS = 4
+VMEM_BYTES = 32 * 2**20
 MESH = pl.DeviceIdType.MESH
 F32, BF16 = jnp.float32, jnp.bfloat16
 ROWS = (48, 48, 48, 48)
@@ -194,8 +195,9 @@
             arrived('s2p', 0, m, j, s2_in[m].at[0, :, low(j)])
             arrived('s2m', 0, m, j, s2_in[m].at[1, :, high(j)])
         total = total + s2_in[m][0, :, cols].astype(F32) + s2_in[m][1, :, cols].astype(F32)
+        new = jnp.minimum(total, 1.0).astype(BF16)
         if t == SQUARINGS - 1:
-            s1_in[m][:, cols] = total.astype(BF16)
+            s1_in[m][:, cols] = new
             left[m] -= 1
             if left[m] == 0:
                 full = s1_in[m][...]
@@ -203,7 +205,6 @@
                 out_ref[span(m), :] = jnp.concatenate(parts, axis=1)
         else:
             slot = (t + 1) % 2
-            new = jnp.minimum(total, 1.0).astype(BF16)
             flush(('xp', 'xm', 'x2', 'co'), m, j)
             b_all[slot, r, span(m), cols] = new
             share(slot, m, j)
@@ -278,15 +279,14 @@
         scratch += each(lambda rows: (rows, width)) + each(lambda rows: (2, rows, width)) + each(lambda rows: (rows, width))
         if FAR_SUMS:
             scratch += each(lambda rows: (rows, width))
-        total = pl.pallas_call(
+        return pl.pallas_call(
             kernel,
             out_shape=jax.ShapeDtypeStruct((slab, width), BF16),
             in_specs=[pl.BlockSpec(memory_space=pltpu.VMEM)],
             out_specs=pl.BlockSpec(memory_space=pltpu.VMEM),
             scratch_shapes=scratch,
-            compiler_params=pltpu.CompilerParams(collective_id=0, has_side_effects=True),
+            compiler_params=pltpu.CompilerParams(collective_id=0, has_side_effects=True, vmem_limit_bytes=VMEM_BYTES),
         )(row_slab)
-        return jnp.minimum(total.astype(F32), 1.0).astype(BF16)
 
     layout = P(('row', 'depth'), 'col')
     return jax.shard_map(local, mesh=mesh, in_specs=(layout,), out_specs=layout, check_vma=False)

time: 149 us -> 146 us (0.980)
  Pallas kernels: 146 us -> 144 us
  other arithmetic: 1.97 us -> 0 us
  local copies, waits for them, and re-layouts: 0 us -> 1.88 us
    pallas_call x1, Pallas kernels: 146 us -> 144 us  [local(): pl.pallas_call(kernel, out_shape=jax.ShapeDtypeStruct((slab, width), BF16...]
    convert_element_type x1 -> x0, other arithmetic: 1.97 us -> none  [local(): return jnp.minimum(total.astype(F32), 1.0).astype(BF16)]
    unnamed x0 -> x3, local copies, waits for them, and re-layouts: none -> 1.88 us
where the time goes in v10:
time: 146 us; the launch traced here: 145 us
  Pallas kernels  144 us (99%)
  local copies, waits for them, and re-layouts  1.88 us (1%)
    pallas_call x1, Pallas kernels, local(): pl.pallas_call(kernel, out_shape=jax.ShapeDtypeStruct((slab, width), BF16...  144 us

profile of v10, /device:TPU:1, one launch (start us, length us, event | category | flops | bytes accessed | tf_op | source)
XLA Modules:
  0.0 145.4 jit_solution(8353857538594551383)
XLA Ops:
  0.0 0.0 copy-start
  0.0 1.1 copy-done
  1.1 143.6 %shard_map.17 = bf16[192,1536]{1,0:T(8,128)(2,1)S(1)} custom-call(bf16[192,1536]{1,0:T(8,128)(2,1)S(1)} %copy-done), custom_call_target="tpu_custom_call" | custom-call | tf_op jit(solution)/shard_map/pallas_call | solution.py:282
  144.6 0.8 copy.3
Async XLA Ops:
  0.0 1.1 copy-start

commit v11 on v10

--- a/solution.py
+++ b/solution.py
@@ -19,14 +19,14 @@
 COL_NAMES = ('a1', 'a2', 'a3', 'yp', 'ym', 'yfp', 'yfm')
 SENDS = 48
 ORDER = (
-    'I1I0A0I3I7I5I6A3G1Y0Y3G7G3G5I2A1Z0I4A2H7Z3H3G6H1H5G0Y1B1C1G2',
-    'Y2G4C7S1Z1H6H2H0H4S7B0C6C0Z2F1C2S6S0G1C4F7S2F6A3S4F0A0C5C3F2',
-    'Y3G7F4S5Y0G2G0G6S3Z3G4F5A2H1F3H0H2H7Z0A1H6H4B0G5Y2C6G3C0Y1H3',
-    'H5S6Z2S0B1C1C7Z1F0F6S1C4S7C2S4G0F1A0F7S2A3G6C3F4Y0G1C5F2Y3S3',
-    'G4S5G7G2Z0F3A1F5H1H0Z3H6H7H2H4A2G3B0Y1C0G5C6H3Y2S0H5Z1S6B1C1',
-    'C7Z2S1C3F0S7C5F6S3F1A0S5F7A3G0C4F3Y0G6C2F5G7G1Y3S4S2G3Z0G5F4',
-    'A2F2H3A1Z3H7H1H5G4B1Y2C1G2C7Y1H6H0S1H2H4Z2S7B0C6C0Z1S6C5S0F1',
-    'C3F6C2C4S5F0S2S3S4F2F5F3F7F4',
+    'I1I0A0I5I2I7I3A1I6A3Y0G5Y1G7Y3G1G3G2I4A2Z1H5H7Z0G0H1Z3H3G6Y2',
+    'B1C3H2G4C1C7H6H0H4S3B0C2Z2C6S2S7F3S6C5F2A1S1G3F6S5F7A3C0Y1F1',
+    'C4F5G7Y3H3S0G1G6S4G5Z1F0A0H7H1F4A2H5G2Z3B1C3G0Y0G4H2H6C7H0Y2',
+    'S3H4B0C6Z0C2F3S7Z2S6S2C0G3C4F2A1F6S0F7S4A3C1G2Y1F0C5F4G6Y3S1',
+    'G0S5G4F1H2H6Z1F5A2Z3H0H4A0G7B0G1C2G5Y2H7C6Y0H3H1S2H5B1C7C3S6',
+    'Z2S7S3Z0F2C4F6F7A3C5C0G6G2S4Y3S5F3A1S0G7F4F5A2Z3C1Y1F0G4G3Y2',
+    'S1G0Z1H4H6F1A0H2H0G5B0Z2C6G1C2H3H5Y0H7S6C4H1S2B1C5Z0S4C3C7S5',
+    'C0F2C1S3S7S0F4F5S1F3F0F6F7F1',
 )
 
 

time: 146 us -> 148 us (1.014)
  Pallas kernels: 144 us -> 146 us
    pallas_call x1, Pallas kernels: 144 us -> 146 us  [local(): pl.pallas_call(kernel, out_shape=jax.ShapeDtypeStruct((slab, width), BF16...]
where the time goes in v11:
time: 148 us; the launch traced here: 147 us
  Pallas kernels  146 us (99%)
  local copies, waits for them, and re-layouts  1.88 us (1%)
    pallas_call x1, Pallas kernels, local(): pl.pallas_call(kernel, out_shape=jax.ShapeDtypeStruct((slab, width), BF16...  146 us

profile of v11, /device:TPU:1, one launch (start us, length us, event | category | flops | bytes accessed | tf_op | source)
XLA Modules:
  0.0 147.4 jit_solution(4648363524988273807)
XLA Ops:
  0.0 0.0 copy-start
  0.0 1.1 copy-done
  1.1 145.5 %shard_map.17 = bf16[192,1536]{1,0:T(8,128)(2,1)S(1)} custom-call(bf16[192,1536]{1,0:T(8,128)(2,1)S(1)} %copy-done), custom_call_target="tpu_custom_call" | custom-call | tf_op jit(solution)/shard_map/pallas_call | solution.py:282
  146.6 0.8 copy.3
Async XLA Ops:
  0.0 1.1 copy-start

commit v12 on v11

--- a/solution.py
+++ b/solution.py
@@ -19,14 +19,14 @@
 COL_NAMES = ('a1', 'a2', 'a3', 'yp', 'ym', 'yfp', 'yfm')
 SENDS = 48
 ORDER = (
-    'I1I0A0I5I2I7I3A1I6A3Y0G5Y1G7Y3G1G3G2I4A2Z1H5H7Z0G0H1Z3H3G6Y2',
-    'B1C3H2G4C1C7H6H0H4S3B0C2Z2C6S2S7F3S6C5F2A1S1G3F6S5F7A3C0Y1F1',
-    'C4F5G7Y3H3S0G1G6S4G5Z1F0A0H7H1F4A2H5G2Z3B1C3G0Y0G4H2H6C7H0Y2',
-    'S3H4B0C6Z0C2F3S7Z2S6S2C0G3C4F2A1F6S0F7S4A3C1G2Y1F0C5F4G6Y3S1',
-    'G0S5G4F1H2H6Z1F5A2Z3H0H4A0G7B0G1C2G5Y2H7C6Y0H3H1S2H5B1C7C3S6',
-    'Z2S7S3Z0F2C4F6F7A3C5C0G6G2S4Y3S5F3A1S0G7F4F5A2Z3C1Y1F0G4G3Y2',
-    'S1G0Z1H4H6F1A0H2H0G5B0Z2C6G1C2H3H5Y0H7S6C4H1S2B1C5Z0S4C3C7S5',
-    'C0F2C1S3S7S0F4F5S1F3F0F6F7F1',
+    'I0I1A0I3I5I7I6A3Y0Y3G1G5G3G7I2A1I4Z0A2G0G6Z3H3H5H1H7Y1B1C1G2',
+    'C7G4Y2S1Z1H2H0H6H4S7B0C6C0Z2F7F1S6C2S0C4F6A3G1S2G7S4F0A0G6C5',
+    'Y3F2C3H1F4G0Y0S5G2S3Z3G4F5A2H0H6H2F3A1H4Z0B0C6G5Y2G3H7C0S6Y1',
+    'H5H3B1C1Z2C7F6S0Z1S1S7C4G6C2F1F0A0S4S2F7A3C3G0Y0F4C5F2Y3S3G1',
+    'G4S5G7Z0G2F3A1H4H6F5H0H1Z3H2A2B0C0Y1G3G5C6H7S0Y2H5H3S6B1Z1C1',
+    'F0C7Z2F6S1C3S7G0C5F1A0G6S3F7S5A3C4G1Y0F3C2F5G7Y3S4G3S2Z0G5H1',
+    'H0F4A2H3F2H5H7A1Z3B1C1G4Y2G2C7Y1H4S1H6H2B0C0Z2C6S0S7Z1S6C4F1',
+    'C5C3C2S5F6S3S4F0S2F3F7F4F5F2',
 )
 
 

time: 148 us -> 148 us (level)
  no operation moved by 1% of the time
where the time goes in v12:
time: 148 us
  Pallas kernels  146 us (99%)
  local copies, waits for them, and re-layouts  1.88 us (1%)
    pallas_call x1, Pallas kernels, local(): pl.pallas_call(kernel, out_shape=jax.ShapeDtypeStruct((slab, width), BF16...  146 us

profile of v12, /device:TPU:1, one launch (start us, length us, event | category | flops | bytes accessed | tf_op | source)
XLA Modules:
  0.0 147.7 jit_solution(17516394495376335627)
XLA Ops:
  0.0 0.0 copy-start
  0.0 1.1 copy-done
  1.1 145.8 %shard_map.17 = bf16[192,1536]{1,0:T(8,128)(2,1)S(1)} custom-call(bf16[192,1536]{1,0:T(8,128)(2,1)S(1)} %copy-done), custom_call_target="tpu_custom_call" | custom-call | tf_op jit(solution)/shard_map/pallas_call | solution.py:282
  146.9 0.8 copy.3
Async XLA Ops:
  0.0 1.1 copy-start

commit v13 on v12

--- a/solution.py
+++ b/solution.py
@@ -12,21 +12,21 @@
 ROWS = (48, 48, 48, 48)
 COLS = (768, 768)
 TILE = 768
-FAR_ROWS = ()
+FAR_ROWS = ((3, 0), (3, 1))
 FAR_SUMS = ()
 SUM_NAMES = ('s1p', 's1m', 'dp', 'dm', 's2p', 's2m')
-ROW_NAMES = ('xp', 'xm', 'xfp', 'xfm', 'co', 'cl', 'cr', 'cx')
+ROW_NAMES = ('xp', 'xm', 'xfp', 'xfm', 'co', 'cl', 'cr', 'cx', 'x2')
 COL_NAMES = ('a1', 'a2', 'a3', 'yp', 'ym', 'yfp', 'yfm')
 SENDS = 48
 ORDER = (
-    'I0I1A0I3I5I7I6A3Y0Y3G1G5G3G7I2A1I4Z0A2G0G6Z3H3H5H1H7Y1B1C1G2',
-    'C7G4Y2S1Z1H2H0H6H4S7B0C6C0Z2F7F1S6C2S0C4F6A3G1S2G7S4F0A0G6C5',
-    'Y3F2C3H1F4G0Y0S5G2S3Z3G4F5A2H0H6H2F3A1H4Z0B0C6G5Y2G3H7C0S6Y1',
-    'H5H3B1C1Z2C7F6S0Z1S1S7C4G6C2F1F0A0S4S2F7A3C3G0Y0F4C5F2Y3S3G1',
-    'G4S5G7Z0G2F3A1H4H6F5H0H1Z3H2A2B0C0Y1G3G5C6H7S0Y2H5H3S6B1Z1C1',
-    'F0C7Z2F6S1C3S7G0C5F1A0G6S3F7S5A3C4G1Y0F3C2F5G7Y3S4G3S2Z0G5H1',
-    'H0F4A2H3F2H5H7A1Z3B1C1G4Y2G2C7Y1H4S1H6H2B0C0Z2C6S0S7Z1S6C4F1',
-    'C5C3C2S5F6S3S4F0S2F3F7F4F5F2',
+    'I4I0I2I5A2I3A1Y2Y1G0G4I6G2I1A0I7Z2G3Y0A3G6Z1H6H0H4H2Z0B0C4G1',
+    'G5C2C0H3G7H7S4Y3H1S2H5B1S0C3F4C5Z3F2S3C1F0S5F3A1S1G2C6G4F5A2',
+    'Y1F1G3G0S6C7G5Y2F6S7H4H2Z1H3A0G1F7H5A3G6Z2Y0H0H6B0C2H1Y3C4G7',
+    'H7B1S2Z0C5C3F2S5S4Z3C1S3F5F4A2C7F3S1A1G5G2Y2S7C0F1C6G3F7Y1S0',
+    'Z2G1S6G4F0A0F6A3H5Z1G7H3H7H2H1B1Y0C5G0C3Y3G6H6H4S5H0S3Z0B0C4',
+    'C2F5S4C1S2Z3F3F4A2S1G5C0C7F2Y2F1S0A1H5G3S7F0A0Z2C6Y1G1F7Y0G2',
+    'S6G0G4G7F6A3H1H3Z1H7B1Z0C5H2C3H0Y3H4G6S5C1H6S3B0C0C2Z3C4S1F3',
+    'S2F5C7C6S4S0S6F1S7F2F4F0F6F7',
 )
 
 

time: 148 us -> 150 us (1.014)
  Pallas kernels: 146 us -> 148 us
    pallas_call x1, Pallas kernels: 146 us -> 148 us  [local(): pl.pallas_call(kernel, out_shape=jax.ShapeDtypeStruct((slab, width), BF16...]
where the time goes in v13:
time: 150 us
  Pallas kernels  148 us (99%)
  local copies, waits for them, and re-layouts  1.88 us (1%)
    pallas_call x1, Pallas kernels, local(): pl.pallas_call(kernel, out_shape=jax.ShapeDtypeStruct((slab, width), BF16...  148 us

profile of v13, /device:TPU:1, one launch (start us, length us, event | category | flops | bytes accessed | tf_op | source)
XLA Modules:
  0.0 149.9 jit_solution(17404832210545917201)
XLA Ops:
  0.0 0.0 copy-start
  0.0 1.1 copy-done
  1.1 148.0 %shard_map.17 = bf16[192,1536]{1,0:T(8,128)(2,1)S(1)} custom-call(bf16[192,1536]{1,0:T(8,128)(2,1)S(1)} %copy-done), custom_call_target="tpu_custom_call" | custom-call | tf_op jit(solution)/shard_map/pallas_call | solution.py:282
  149.1 0.8 copy.3
Async XLA Ops:
  0.0 1.1 copy-start

commit v14 on v12

--- a/solution.py
+++ b/solution.py
@@ -19,14 +19,14 @@
 COL_NAMES = ('a1', 'a2', 'a3', 'yp', 'ym', 'yfp', 'yfm')
 SENDS = 48
 ORDER = (
-    'I0I1A0I3I5I7I6A3Y0Y3G1G5G3G7I2A1I4Z0A2G0G6Z3H3H5H1H7Y1B1C1G2',
-    'C7G4Y2S1Z1H2H0H6H4S7B0C6C0Z2F7F1S6C2S0C4F6A3G1S2G7S4F0A0G6C5',
-    'Y3F2C3H1F4G0Y0S5G2S3Z3G4F5A2H0H6H2F3A1H4Z0B0C6G5Y2G3H7C0S6Y1',
-    'H5H3B1C1Z2C7F6S0Z1S1S7C4G6C2F1F0A0S4S2F7A3C3G0Y0F4C5F2Y3S3G1',
-    'G4S5G7Z0G2F3A1H4H6F5H0H1Z3H2A2B0C0Y1G3G5C6H7S0Y2H5H3S6B1Z1C1',
-    'F0C7Z2F6S1C3S7G0C5F1A0G6S3F7S5A3C4G1Y0F3C2F5G7Y3S4G3S2Z0G5H1',
-    'H0F4A2H3F2H5H7A1Z3B1C1G4Y2G2C7Y1H4S1H6H2B0C0Z2C6S0S7Z1S6C4F1',
-    'C5C3C2S5F6S3S4F0S2F3F7F4F5F2',
+    'I3I1I5I7I0I6A0I4A2A3Y0G3G1G5Y2G7I2A1Y3Z2Z0H3G6G4H5Z3H1G0H7Y1',
+    'B1C5G2C1C7H0H4S5H6H2S1B0C0Z1S7C4S0F5C3F1F7S4F0A0S3F4A2C6Y0F3',
+    'C2G7Y2G5S6G1G0S2Z0G3F6A3F2H7Z2A1H5G4H1H3Y3H0B1G6C1G2Y1C5H6S1',
+    'H4H2Z3S5B0C4C0Z1F1C7F5S4S0C3S7F4G5F0A0S3A2C6F7C2Y0F3G4G1Y2S6',
+    'S2G7Z0G3F6A3F2H4Z2G0H1H5A1H7H3Y3B1G6C1G2C5S1H6H0Z3Y1H2S5B0C0',
+    'C4C7F5F1S4S0Z1C6F4A2S7S6G5C2G1F0A0F6Y2S2F7A3C3G4Y0H1F2Y3G7G6',
+    'Z2S3G0G2Z0F3H6H4A1H0H5Z3H2B0C4G3C0H7Y1C6S4H3S0B1C1C7Z1F4S6S1',
+    'C5C3C2S5S7S2S3F1F5F6F0F7F2F3',
 )
 
 

time: 148 us -> 150 us (1.014)
  Pallas kernels: 146 us -> 148 us
    pallas_call x1, Pallas kernels: 146 us -> 148 us  [local(): pl.pallas_call(kernel, out_shape=jax.ShapeDtypeStruct((slab, width), BF16...]
where the time goes in v14:
time: 150 us; the launch traced here: 149 us
  Pallas kernels  148 us (99%)
  local copies, waits for them, and re-layouts  1.88 us (1%)
    pallas_call x1, Pallas kernels, local(): pl.pallas_call(kernel, out_shape=jax.ShapeDtypeStruct((slab, width), BF16...  148 us

profile of v14, /device:TPU:1, one launch (start us, length us, event | category | flops | bytes accessed | tf_op | source)
XLA Modules:
  0.0 149.4 jit_solution(4524953093958863527)
XLA Ops:
  0.0 0.0 copy-start
  0.0 1.1 copy-done
  1.1 147.5 %shard_map.17 = bf16[192,1536]{1,0:T(8,128)(2,1)S(1)} custom-call(bf16[192,1536]{1,0:T(8,128)(2,1)S(1)} %copy-done), custom_call_target="tpu_custom_call" | custom-call | tf_op jit(solution)/shard_map/pallas_call | solution.py:282
  148.6 0.8 copy.3
Async XLA Ops:
  0.0 1.1 copy-start

commit v15 on v10

--- a/solution.py
+++ b/solution.py
@@ -17,7 +17,7 @@
 SUM_NAMES = ('s1p', 's1m', 'dp', 'dm', 's2p', 's2m')
 ROW_NAMES = ('xp', 'xm', 'xfp', 'xfm', 'co', 'cl', 'cr', 'cx')
 COL_NAMES = ('a1', 'a2', 'a3', 'yp', 'ym', 'yfp', 'yfm')
-SENDS = 48
+SENDS = 160
 ORDER = (
     'I1I0A0I3I7I5I6A3G1Y0Y3G7G3G5I2A1Z0I4A2H7Z3H3G6H1H5G0Y1B1C1G2',
     'Y2G4C7S1Z1H6H2H0H4S7B0C6C0Z2F1C2S6S0G1C4F7S2F6A3S4F0A0C5C3F2',

time: 146 us -> 147 us (level)
  no operation moved by 1% of the time
where the time goes in v15:
time: 147 us; the launch traced here: 146 us
  Pallas kernels  144 us (98%)
  local copies, waits for them, and re-layouts  1.88 us (1%)
    pallas_call x1, Pallas kernels, local(): pl.pallas_call(kernel, out_shape=jax.ShapeDtypeStruct((slab, width), BF16...  144 us

profile of v15, /device:TPU:1, one launch (start us, length us, event | category | flops | bytes accessed | tf_op | source)
XLA Modules:
  0.0 146.4 jit_solution(15984010769229709731)
XLA Ops:
  0.0 0.0 copy-start
  0.0 1.1 copy-done
  1.1 144.5 %shard_map.17 = bf16[192,1536]{1,0:T(8,128)(2,1)S(1)} custom-call(bf16[192,1536]{1,0:T(8,128)(2,1)S(1)} %copy-done), custom_call_target="tpu_custom_call" | custom-call | tf_op jit(solution)/shard_map/pallas_call | solution.py:282
  145.6 0.8 copy.3
Async XLA Ops:
  0.0 1.1 copy-start

commit v16 on v10

--- a/solution.py
+++ b/solution.py
@@ -11,7 +11,7 @@
 F32, BF16 = jnp.float32, jnp.bfloat16
 ROWS = (48, 48, 48, 48)
 COLS = (768, 768)
-TILE = 768
+TILE = 256
 FAR_ROWS = ()
 FAR_SUMS = ()
 SUM_NAMES = ('s1p', 's1m', 'dp', 'dm', 's2p', 's2m')

time: 146 us -> 149 us (1.021)
  Pallas kernels: 144 us -> 146 us
    pallas_call x1, Pallas kernels: 144 us -> 146 us  [local(): pl.pallas_call(kernel, out_shape=jax.ShapeDtypeStruct((slab, width), BF16...]
where the time goes in v16:
time: 149 us; the launch traced here: 148 us
  Pallas kernels  146 us (98%)
  local copies, waits for them, and re-layouts  1.88 us (1%)
    pallas_call x1, Pallas kernels, local(): pl.pallas_call(kernel, out_shape=jax.ShapeDtypeStruct((slab, width), BF16...  146 us

profile of v16, /device:TPU:1, one launch (start us, length us, event | category | flops | bytes accessed | tf_op | source)
XLA Modules:
  0.0 148.1 jit_solution(15879754858429944111)
XLA Ops:
  0.0 0.0 copy-start
  0.0 1.1 copy-done
  1.1 146.2 %shard_map.17 = bf16[192,1536]{1,0:T(8,128)(2,1)S(1)} custom-call(bf16[192,1536]{1,0:T(8,128)(2,1)S(1)} %copy-done), custom_call_target="tpu_custom_call" | custom-call | tf_op jit(solution)/shard_map/pallas_call | solution.py:282
  147.3 0.8 copy.3
Async XLA Ops:
  0.0 1.1 copy-start
